TPU v7x, 128 devices: a whole 4x4x4 slice. The times are simulated.
128 devices in a mesh: gx: 8 (over x, core), gy: 16 (over y, z).
Axes of the slice: x: 4, y: 4, z: 4, core: 2. Of those that a mesh axis runs over, the one named last changes fastest.
Arguments:
- fine_start: float32 [3, 2048, 8192], P(None, 'gx', 'gy'), may hold values from -6 to 6
- fine_known: float32 [3, 2048, 8192], P(None, 'gx', 'gy'), may hold values from -18 to 18
- fine_mu: float32 [2048, 8192], P('gx', 'gy'), may hold values from 1 to 10
- coarse_start: float32 [3, 1024, 4096], P(None, ('gx', 'gy')), may hold values from -6 to 6
- coarse_known: float32 [3, 1024, 4096], P(None, ('gx', 'gy')), may hold values from -18 to 18
- coarse_mu: float32 [1024, 4096], P(('gx', 'gy')), may hold values from 1 to 10
Outputs:
- fine_ghost: float32 [3, 2048, 8192], P(None, 'gx', 'gy')
- coarse_ghost: float32 [3, 1024, 4096], P(None, ('gx', 'gy'))
- norms: float32 [3], replicated
All inputs are finite; a program needn't handle non-finite values.
Results may differ from a plain program's by a relative error of at most 0.0001.
Values sent between devices are 32-bit elements; how exact they have to be, the bound alone decides.
A program may use at most 128 MiB of HBM per device.

v0:
```python
import functools

import jax
import jax.numpy as jnp
from jax import lax
from jax.experimental import pallas as pl
from jax.experimental.pallas import tpu as pltpu
from jax.sharding import PartitionSpec as P

MESH = pl.DeviceIdType.MESH
F32 = jnp.float32
SWEEPS = 3
LANES = 128
SUB = 8
FINE_OFF = 24
COARSE_OFF = 16
EDGE = 4


class Shape:
    def __init__(self, gx, gy, fine_rows, fine_cols):
        self.gx, self.gy = gx, gy
        self.fine_rows, self.fine_cols = fine_rows, fine_cols
        self.coarse_rows, self.coarse_cols = fine_rows // 2, fine_cols // 2
        self.tiles = self.coarse_rows // SUB
        self.slabs = fine_cols // LANES
        self.halo = self.slabs
        self.all_slabs = self.slabs + 1
        self.wide = self.coarse_cols
        self.fine_buf = fine_rows + 2 * FINE_OFF
        self.coarse_buf = self.coarse_rows + 2 * COARSE_OFF
        self.blocks = fine_rows // LANES
        self.cells = 3.0 * gx * gy * fine_rows * fine_cols * 1.25


def lane_iota():
    return lax.broadcasted_iota(jnp.int32, (SUB, LANES), 1)


def kernel(
    sh,
    fine_start,
    fine_known,
    fine_mu,
    coarse_start,
    coarse_known,
    coarse_mu,
    fine_out,
    coarse_out,
    norm_out,
    f_a,
    f_b,
    kn,
    mu,
    fd,
    fi,
    c_a,
    c_b,
    q_a,
    q_b,
    w_a,
    w_b,
    ck,
    cd,
    ci,
    pre,
    own,
    pack,
    got_c,
    got_p,
    got_k,
    edge_out,
    edge_in,
    fin,
    part,
    part_gy,
    part_gx,
    load_sem,
    edge_send,
    edge_recv,
    row_send,
    row_recv,
    a_send,
    a_recv,
    fwd_send,
    fwd_recv,
    fin_send,
    fin_recv,
    out_sem,
    norm_send,
    norm_recv_y,
    norm_recv_x,
):
    gx, gy = sh.gx, sh.gy
    i = lax.axis_index("gx")
    j = lax.axis_index("gy")
    halo, slabs, tiles = sh.halo, sh.slabs, sh.tiles
    wide = sh.wide
    lane = lane_iota()
    even = lane % 2 == 0
    first = lane == 0
    last = lane == LANES - 1

    def remote(src, dst, send, recv, to_i, to_j):
        return pltpu.make_async_remote_copy(
            src_ref=src,
            dst_ref=dst,
            send_sem=send,
            recv_sem=recv,
            device_id=(to_i, to_j),
            device_id_type=MESH,
        )

    loads = []

    def load(src, dst):
        copy = pltpu.make_async_copy(src, dst, load_sem.at[len(loads)])
        copy.start()
        loads.append(copy)
        return copy

    own_loads = [
        load(coarse_start, own.at[pl.ds(0, 3)]),
        load(coarse_known, own.at[pl.ds(3, 3)]),
        load(coarse_mu, own.at[6]),
    ]
    rows_in = pl.ds(FINE_OFF, sh.fine_rows)
    fine_loads = []
    for t in [halo - 1, 0] + list(range(1, slabs - 1)):
        cols = pl.ds(LANES * t, LANES)
        fine_loads.append(load(fine_start.at[:, :, cols], f_a.at[:, t, rows_in, :]))
        fine_loads.append(load(fine_known.at[:, :, cols], kn.at[:, t, rows_in, :]))
        fine_loads.append(load(fine_mu.at[:, cols], mu.at[t, rows_in, :]))

    zero = jnp.zeros((SUB, LANES), F32)
    fine_end = FINE_OFF + sh.fine_rows

    def zero_fine(step, carry):
        for row in (0, 8, 16, fine_end, fine_end + 8, fine_end + 16):
            rows = pl.ds(row, SUB)
            mu[step, rows, :] = zero
            for k in range(3):
                f_a[k, step, rows, :] = zero
                f_b[k, step, rows, :] = zero
                kn[k, step, rows, :] = zero
        for row in (0, 8, sh.coarse_buf - 16, sh.coarse_buf - 8):
            rows = pl.ds(row, SUB)
            for k in range(3):
                for ref in (c_a, c_b, q_a, q_b):
                    ref[k, step, rows, :] = zero
        return carry

    lax.fori_loop(0, sh.all_slabs, zero_fine, 0)
    for side in range(2):
        for p in range(7):
            edge_in[side, p] = zero
    for slot in (0, gy + 1):
        got_p[slot] = zero
        for u in range(wide // LANES):
            cols = pl.ds(LANES * u, LANES)
            for p in range(3):
                got_c[slot, p, :, cols] = zero
            for p in range(4):
                got_k[slot, p, :, cols] = zero

    barrier = pltpu.get_barrier_semaphore()
    for step in range(1, gy):
        pl.semaphore_signal(
            barrier, inc=1, device_id=(i, lax.rem(j + step, gy)), device_id_type=MESH
        )
    for step in range(1, gx):
        pl.semaphore_signal(
            barrier, inc=1, device_id=(lax.rem(i + step, gx), j), device_id_type=MESH
        )

    for copy in own_loads:
        copy.wait()

    def pack_for(dest, carry):
        after = pl.multiple_of(lax.rem(dest + 1, gy) * wide, LANES)
        before = pl.multiple_of(lax.rem(dest + gy - 1, gy) * wide + wide - LANES, LANES)
        keep_after = jnp.where(dest < gy - 1, 1.0, 0.0).astype(F32)
        keep_before = jnp.where(dest > 0, 1.0, 0.0).astype(F32)
        keep = jnp.where(lane < 64, keep_after, keep_before)
        tile = zero
        for p in range(7):
            both = jnp.where(
                lane < 64, own[p, :, pl.ds(after, LANES)], own[p, :, pl.ds(before, LANES)]
            )
            both = pltpu.roll(both * keep, 8 * p + EDGE, 1)
            here = (lane >= 8 * p) & (lane < 8 * p + 8)
            tile = jnp.where(here, both, tile)
        pack[dest] = tile
        return carry

    lax.fori_loop(0, gy, pack_for, 0)

    for copy in fine_loads:
        copy.wait()

    def planes():
        return [(f_a, k) for k in range(3)] + [(kn, k) for k in range(3)] + [(mu, None)]

    def slab_of(ref, k, t, rows):
        return ref[t, rows, :] if k is None else ref[k, t, rows, :]

    for p, (ref, k) in enumerate(planes()):
        for b in range(sh.blocks):
            rows = pl.ds(FINE_OFF + LANES * b, LANES)
            to_right = slab_of(ref, k, slabs - 1, rows).T
            to_left = slab_of(ref, k, 0, rows).T
            edge_out[0, p, pl.ds(EDGE * b, EDGE), :] = to_right[LANES - EDGE :, :]
            edge_out[1, p, pl.ds(EDGE * b, EDGE), :] = to_left[:EDGE, :]

    pl.semaphore_wait(barrier, gy + gx - 2)

    edge_right = remote(
        edge_out.at[0], edge_in.at[0], edge_send.at[0], edge_recv.at[0], i, lax.rem(j + 1, gy)
    )
    edge_left = remote(
        edge_out.at[1], edge_in.at[1], edge_send.at[1], edge_recv.at[1], i, lax.rem(j + gy - 1, gy)
    )

    @pl.when(j < gy - 1)
    def _():
        edge_right.start()

    @pl.when(j > 0)
    def _():
        edge_left.start()

    def sends_first(step):
        to = lax.rem(j + step, gy)
        from_ = lax.rem(j + gy - step, gy)
        cols = pl.ds(pl.multiple_of(to * wide, LANES), wide)
        return (
            remote(
                own.at[pl.ds(0, 3), :, cols],
                got_c.at[j + 1],
                a_send.at[0, step],
                a_recv.at[0, step],
                i,
                to,
            ),
            remote(pack.at[to], got_p.at[j + 1], a_send.at[1, step], a_recv.at[1, step], i, to),
        )

    def sends_second(step):
        to = lax.rem(j + step, gy)
        cols = pl.ds(pl.multiple_of(to * wide, LANES), wide)
        return remote(
            own.at[pl.ds(3, 4), :, cols],
            got_k.at[j + 1],
            a_send.at[2, step],
            a_recv.at[2, step],
            i,
            to,
        )

    order = list(range(1, gy))
    firsts = {step: sends_first(step) for step in order}
    seconds = {step: sends_second(step) for step in order}
    for step in order:
        firsts[step][0].start()
        firsts[step][1].start()
    for step in order:
        seconds[step].start()

    got_p[j + 1] = pack[j]
    for u in range(wide // LANES):
        cols = pl.ds(pl.multiple_of(j * wide + LANES * u, LANES), LANES)
        for p in range(7):
            piece = own[p, :, cols]
            if p < 3:
                got_c[j + 1, p, :, pl.ds(LANES * u, LANES)] = piece
            else:
                got_k[j + 1, p - 3, :, pl.ds(LANES * u, LANES)] = piece

    @pl.when(j > 0)
    def _():
        edge_right.wait_recv()

    @pl.when(j < gy - 1)
    def _():
        edge_left.wait_recv()

    between = jnp.zeros((LANES - 2 * EDGE, LANES), F32)
    for p, (ref, k) in enumerate(planes()):
        for b in range(sh.blocks):
            from_left = edge_in[0, p, pl.ds(EDGE * b, EDGE), :]
            from_right = edge_in[1, p, pl.ds(EDGE * b, EDGE), :]
            slab = jnp.concatenate([from_right, between, from_left], axis=0).T
            rows = pl.ds(FINE_OFF + LANES * b, LANES)
            if k is None:
                ref[halo, rows, :] = slab
            else:
                ref[k, halo, rows, :] = slab

    down_i, up_i = lax.rem(i + 1, gx), lax.rem(i + gx - 1, gx)
    lo_src, hi_src = pl.ds(FINE_OFF, SUB), pl.ds(fine_end - SUB, SUB)
    lo_dst, hi_dst = pl.ds(FINE_OFF - SUB, SUB), pl.ds(fine_end, SUB)

    def row_copies(src, dst, direction, to_i):
        made = []
        for n, ref in enumerate((f_a, kn)):
            made.append(
                remote(
                    ref.at[:, :, src, :],
                    ref.at[:, :, dst, :],
                    row_send.at[direction, n],
                    row_recv.at[direction, n],
                    to_i,
                    j,
                )
            )
        made.append(
            remote(
                mu.at[:, src, :],
                mu.at[:, dst, :],
                row_send.at[direction, 2],
                row_recv.at[direction, 2],
                to_i,
                j,
            )
        )
        return made

    rows_down = row_copies(hi_src, lo_dst, 0, down_i)
    rows_up = row_copies(lo_src, hi_dst, 1, up_i)

    @pl.when(i < gx - 1)
    def _():
        for copy in rows_down:
            copy.start()

    @pl.when(i > 0)
    def _():
        for copy in rows_up:
            copy.start()

    has_up, has_down = i > 0, i < gx - 1
    has_left, has_right = j > 0, j < gy - 1
    pair = lane // 2

    def spread_index(p):
        right = 8 * p + EDGE + pair
        left = 8 * p + pair - (LANES - 8) // 2
        return jnp.where(lane < 8, right, jnp.where(lane >= LANES - 8, left, 0))

    def take(value, index):
        return jnp.take_along_axis(value, index, axis=1, mode="promise_in_bounds")

    def spread(slot, ref, p, packed_plane):
        out = []
        for t in range(slabs):
            value = ref[slot, p, :, pl.ds(LANES * (t // 2), LANES)]
            out.append(take(value, 64 * (t % 2) + pair))
        out.append(take(got_p[slot], spread_index(packed_plane)))
        return out

    def shifted(values):
        count = len(values)
        right = [pltpu.roll(v, 1, 1) for v in values]
        left = [pltpu.roll(v, LANES - 1, 1) for v in values]
        before = [jnp.where(first, right[t - 1], right[t]) for t in range(count)]
        after = [jnp.where(last, left[(t + 1) % count], left[t]) for t in range(count)]
        return before, after

    def produce(k, row, values, c_ref, q_ref, w_ref):
        before, after = shifted(values)
        rows = pl.ds(row, SUB)
        for t, value in enumerate(values):
            outer = jnp.where(even, before[t], after[t])
            swap = jnp.where(even, pltpu.roll(outer, LANES - 1, 1), pltpu.roll(outer, 1, 1))
            c_ref[k, t, rows, :] = value
            q_ref[k, t, rows, :] = 0.375 * value + 0.125 * outer
            w_ref[k, t, rows, :] = outer + swap

    def coarse_row(m):
        return pl.multiple_of(COARSE_OFF + SUB * m, SUB)

    def spread_first(slot, carry):
        for k in range(3):
            produce(k, coarse_row(slot - 1), spread(slot, got_c, k, k), c_a, q_a, w_a)
        return carry

    halo_lanes = ((lane < 8) & has_right) | ((lane >= LANES - 8) & has_left)
    halo_lanes_fine = ((lane < EDGE) & has_right) | ((lane >= LANES - EDGE) & has_left)

    def spread_second(slot, carry):
        rows = pl.ds(coarse_row(slot - 1), SUB)
        inside = ((slot > 0) | has_up) & ((slot <= gy) | has_down)
        for k in range(3):
            for t, value in enumerate(spread(slot, got_k, k, 3 + k)):
                ck[k, t, rows, :] = value
        for t, value in enumerate(spread(slot, got_k, 3, 6)):
            diag = value + 1.0
            valid = (halo_lanes if t == halo else (lane >= 0)) & inside
            cd[t, rows, :] = diag
            ci[t, rows, :] = jnp.where(valid, 1.0 / diag, 0.0)
        return carry

    fwd_copies = {}
    for n, ref in enumerate((got_c, got_p, got_k)):
        fwd_copies[n] = (
            remote(ref.at[gy], ref.at[0], fwd_send.at[0, n], fwd_recv.at[0, n], down_i, j),
            remote(ref.at[1], ref.at[gy + 1], fwd_send.at[1, n], fwd_recv.at[1, n], up_i, j),
        )

    def wait_from(kinds, source):
        step = lax.rem(j - source + gy, gy)

        @pl.when(step > 0)
        def _():
            for kind in kinds:
                dst = (got_c, got_p, got_k)[kind].at[source + 1]
                pltpu.make_async_remote_copy(
                    src_ref=dst,
                    dst_ref=dst,
                    send_sem=a_send.at[kind, step],
                    recv_sem=a_recv.at[kind, step],
                    device_id=(i, source),
                    device_id_type=MESH,
                ).wait_recv()

    def pass_on(kinds):
        wait_from(kinds, gy - 1)

        @pl.when(has_down)
        def _():
            for kind in kinds:
                fwd_copies[kind][0].start()

        wait_from(kinds, 0)

        @pl.when(has_up)
        def _():
            for kind in kinds:
                fwd_copies[kind][1].start()

        def rest(source, carry):
            wait_from(kinds, source)
            return carry

        lax.fori_loop(1, gy - 1, rest, 0)

    def passed_on(kinds):
        @pl.when(has_up)
        def _():
            for kind in kinds:
                fwd_copies[kind][0].wait_recv()

        @pl.when(has_down)
        def _():
            for kind in kinds:
                fwd_copies[kind][1].wait_recv()

    pass_on((0, 1))
    lax.fori_loop(1, gy + 1, spread_first, 0)

    @pl.when(has_up)
    def _():
        for copy in rows_down:
            copy.wait_recv()

    @pl.when(has_down)
    def _():
        for copy in rows_up:
            copy.wait_recv()

    low_row = jnp.where(has_up, FINE_OFF - SUB, FINE_OFF)
    high_row = jnp.where(has_down, fine_end + SUB, fine_end)

    def diagonals(step, carry):
        row = pl.multiple_of(SUB * (step + 1), SUB)
        rows = pl.ds(row, SUB)
        inside = (row >= low_row) & (row < high_row)
        for t in range(sh.all_slabs):
            diag = mu[t, rows, :] + 1.0
            valid = (halo_lanes_fine if t == halo else (lane >= 0)) & inside
            fd[t, rows, :] = diag
            fi[t, rows, :] = jnp.where(valid, 1.0 / diag, 0.0)
        return carry

    lax.fori_loop(0, sh.fine_buf // SUB - 2, diagonals, 0)

    passed_on((0, 1))
    spread_first(0, 0)
    spread_first(gy + 1, 0)

    def fine_tile(m, acc, f_in, q_ref, f_out, count, out_off):
        base = FINE_OFF + 16 * m
        upper, lower = pl.ds(base, SUB, stride=2), pl.ds(base + 1, SUB, stride=2)
        above, below = pl.ds(base - 1, SUB, stride=2), pl.ds(base + 2, SUB, stride=2)
        crow = COARSE_OFF + SUB * m
        q_here, q_up, q_down = pl.ds(crow, SUB), pl.ds(crow - 1, SUB), pl.ds(crow + 1, SUB)
        out_upper = pl.ds(base + out_off, SUB, stride=2)
        out_lower = pl.ds(base + 1 + out_off, SUB, stride=2)
        for k in range(3):
            tops = [f_in[k, t, upper, :] for t in range(sh.all_slabs)]
            lows = [f_in[k, t, lower, :] for t in range(sh.all_slabs)]
            top_l, top_r = shifted(tops)
            low_l, low_r = shifted(lows)
            for t in range(count):
                three = 3.0 * q_ref[k, t, q_here, :]
                nb = lows[t] + f_in[k, t, above, :] + top_l[t] + top_r[t]
                nb = nb + (three + q_ref[k, t, q_up, :])
                total = kn[k, t, upper, :] + 0.25 * nb
                res = total - fd[t, upper, :] * tops[t]
                f_out[k, t, out_upper, :] = total * fi[t, upper, :]
                nb2 = tops[t] + f_in[k, t, below, :] + low_l[t] + low_r[t]
                nb2 = nb2 + (three + q_ref[k, t, q_down, :])
                total2 = kn[k, t, lower, :] + 0.25 * nb2
                res2 = total2 - fd[t, lower, :] * lows[t]
                f_out[k, t, out_lower, :] = total2 * fi[t, lower, :]
                if acc is not None and t < slabs:
                    acc = acc + (res * res + res2 * res2)
        return acc

    def coarse_sum(m, k, t, f_in, c_ref, w_ref):
        base = FINE_OFF + 16 * m
        crow = COARSE_OFF + SUB * m
        pairs = f_in[k, t, pl.ds(base, SUB, stride=2), :]
        pairs = pairs + f_in[k, t, pl.ds(base + 1, SUB, stride=2), :]
        swap = jnp.where(even, pltpu.roll(pairs, LANES - 1, 1), pltpu.roll(pairs, 1, 1))
        nb = c_ref[k, t, pl.ds(crow - 1, SUB), :] + c_ref[k, t, pl.ds(crow + 1, SUB), :]
        nb = nb + w_ref[k, t, pl.ds(coarse_row(m), SUB), :]
        return 0.25 * (nb + 0.5 * (pairs + swap))

    def coarse_step(m, k, t, acc, added, c_ref):
        rows = pl.ds(coarse_row(m), SUB)
        total = ck[k, t, rows, :] + added
        res = total - cd[t, rows, :] * c_ref[k, t, rows, :]
        if acc is not None and t < slabs:
            acc = acc + res * res
        return total * ci[t, rows, :], acc

    def first_sum(m, carry):
        rows = pl.ds(coarse_row(m), SUB)
        for k in range(3):
            for t in range(sh.all_slabs):
                pre[k, t, rows, :] = coarse_sum(m, k, t, f_a, c_a, w_a)
        return carry

    def first_coarse(m, acc):
        rows = pl.ds(coarse_row(m), SUB)
        for k in range(3):
            values = []
            for t in range(sh.all_slabs):
                value, acc = coarse_step(m, k, t, acc, pre[k, t, rows, :], c_a)
                values.append(value)
            produce(k, coarse_row(m), values, c_b, q_b, w_b)
        return acc

    def second_coarse(m, acc):
        for k in range(3):
            values = []
            for t in range(sh.all_slabs):
                added = coarse_sum(m, k, t, f_b, c_b, w_b)
                value, acc = coarse_step(m, k, t, acc, added, c_b)
                values.append(value)
            produce(k, coarse_row(m), values, c_a, q_a, w_a)
        return acc

    gather_low = jnp.where(lane < 64, 2 * lane, 0)
    gather_high = jnp.where(lane < 64, 0, 2 * lane - LANES)

    def third_coarse(m, acc):
        for k in range(3):
            values = []
            for t in range(slabs):
                added = coarse_sum(m, k, t, f_a, c_a, w_a)
                value, acc = coarse_step(m, k, t, acc, added, c_a)
                values.append(value)
            for u in range(wide // LANES):
                narrow = jnp.where(
                    lane < 64, take(values[2 * u], gather_low), take(values[2 * u + 1], gather_high)
                )
                fin[m, k, :, pl.ds(LANES * u, LANES)] = narrow
        return acc

    def every_tile(body, acc):
        acc = lax.fori_loop(0, tiles, body, acc)
        body(-1, None)
        body(tiles, None)
        return acc

    def fine_first(m, acc):
        return fine_tile(m, acc, f_a, q_a, f_b, sh.all_slabs, 0)

    def fine_second(m, acc):
        return fine_tile(m, acc, f_b, q_b, f_a, sh.all_slabs, 0)

    def fine_third(m, acc):
        return fine_tile(m, acc, f_a, q_a, f_b, slabs, 0)

    fine_sum1 = every_tile(fine_first, zero)
    every_tile(first_sum, 0)

    pass_on((2,))
    lax.fori_loop(1, gy + 1, spread_second, 0)
    passed_on((2,))
    spread_second(0, 0)
    spread_second(gy + 1, 0)

    coarse_sum1 = every_tile(first_coarse, zero)

    @pl.when(has_down)
    def _():
        for copy in rows_down:
            copy.wait_send()

    @pl.when(has_up)
    def _():
        for copy in rows_up:
            copy.wait_send()

    fine_sum2 = every_tile(fine_second, zero)
    coarse_sum2 = every_tile(second_coarse, zero)
    coarse_sum3 = lax.fori_loop(0, tiles, third_coarse, zero)

    my_cols = pl.ds(pl.multiple_of(j * wide, LANES), wide)
    finals = []
    for step in order:
        to = lax.rem(j + step, gy)
        copy = remote(
            fin.at[to],
            coarse_out.at[:, :, my_cols],
            fin_send.at[step],
            fin_recv.at[step],
            i,
            to,
        )
        copy.start()
        finals.append(copy)
    own_final = pltpu.make_async_copy(fin.at[j], coarse_out.at[:, :, my_cols], out_sem.at[slabs])
    own_final.start()

    fine_sum3 = lax.fori_loop(0, tiles, fine_third, zero)
    fine_stores = []
    for t in range(slabs):
        copy = pltpu.make_async_copy(
            f_b.at[:, t, rows_in, :],
            fine_out.at[:, :, pl.ds(LANES * t, LANES)],
            out_sem.at[t],
        )
        copy.start()
        fine_stores.append(copy)

    row_of = lax.broadcasted_iota(jnp.int32, (SUB, LANES), 0)
    mine = zero
    sums = ((fine_sum1, coarse_sum1), (fine_sum2, coarse_sum2), (fine_sum3, coarse_sum3))
    for s, (fine_part, coarse_part) in enumerate(sums):
        line = jnp.sum(fine_part + 0.5 * coarse_part, axis=0, keepdims=True)
        mine = jnp.where(row_of == s, line, mine)
    part[0] = mine
    norm_y = []
    for step in order:
        copy = remote(
            part.at[0],
            part_gy.at[step],
            norm_send.at[0, step],
            norm_recv_y.at[step],
            i,
            lax.rem(j + step, gy),
        )
        copy.start()
        norm_y.append(copy)
    for copy in norm_y:
        copy.wait_recv()
    for step in order:
        mine = mine + part_gy[step]
    part[1] = mine
    norm_x = []
    for step in range(1, gx):
        copy = remote(
            part.at[1],
            part_gx.at[step],
            norm_send.at[1, step],
            norm_recv_x.at[step],
            lax.rem(i + step, gx),
            j,
        )
        copy.start()
        norm_x.append(copy)
    for copy in norm_x:
        copy.wait_recv()
    for step in range(1, gx):
        mine = mine + part_gx[step]
    norms = jnp.sqrt(jnp.sum(mine, axis=1, keepdims=True) * (1.0 / sh.cells))
    for s in range(SWEEPS):
        norm_out[s] = norms[s, 0]

    @pl.when(has_right)
    def _():
        edge_right.wait_send()

    @pl.when(has_left)
    def _():
        edge_left.wait_send()

    @pl.when(has_down)
    def _():
        for kind in range(3):
            fwd_copies[kind][0].wait_send()

    @pl.when(has_up)
    def _():
        for kind in range(3):
            fwd_copies[kind][1].wait_send()

    for step in order:
        for copy in firsts[step]:
            copy.wait_send()
        seconds[step].wait_send()
    for copy in finals:
        copy.wait()
    own_final.wait()
    for copy in fine_stores:
        copy.wait()
    for copy in norm_y + norm_x:
        copy.wait_send()


def solution(mesh):
    gx, gy = mesh.shape["gx"], mesh.shape["gy"]

    def on_device(fine_start, fine_known, fine_mu, coarse_start, coarse_known, coarse_mu):
        sh = Shape(gx, gy, *fine_mu.shape)
        fine = pltpu.VMEM((3, sh.all_slabs, sh.fine_buf, LANES), F32)
        fine_one = pltpu.VMEM((sh.all_slabs, sh.fine_buf, LANES), F32)
        coarse = pltpu.VMEM((3, sh.all_slabs, sh.coarse_buf, LANES), F32)
        coarse_one = pltpu.VMEM((sh.all_slabs, sh.coarse_buf, LANES), F32)
        dma = pltpu.SemaphoreType.DMA
        anywhere = pl.BlockSpec(memory_space=pl.ANY)
        return pl.pallas_call(
            functools.partial(kernel, sh),
            out_shape=(
                jax.ShapeDtypeStruct(fine_start.shape, F32),
                jax.ShapeDtypeStruct(coarse_start.shape, F32),
                jax.ShapeDtypeStruct((SWEEPS,), F32),
            ),
            in_specs=[anywhere] * 6,
            out_specs=(anywhere, anywhere, pl.BlockSpec(memory_space=pltpu.SMEM)),
            scratch_shapes=[
                fine,
                fine,
                fine,
                fine_one,
                fine_one,
                fine_one,
                coarse,
                coarse,
                coarse,
                coarse,
                coarse,
                coarse,
                coarse,
                coarse_one,
                coarse_one,
                coarse,
                pltpu.VMEM((7, SUB, gy * sh.wide), F32),
                pltpu.VMEM((gy, SUB, LANES), F32),
                pltpu.VMEM((gy + 2, 3, SUB, sh.wide), F32),
                pltpu.VMEM((gy + 2, SUB, LANES), F32),
                pltpu.VMEM((gy + 2, 4, SUB, sh.wide), F32),
                pltpu.VMEM((2, 7, SUB, LANES), F32),
                pltpu.VMEM((2, 7, SUB, LANES), F32),
                pltpu.VMEM((gy, 3, SUB, sh.wide), F32),
                pltpu.VMEM((2, SUB, LANES), F32),
                pltpu.VMEM((gy, SUB, LANES), F32),
                pltpu.VMEM((gx, SUB, LANES), F32),
                dma((3 + 3 * sh.slabs,)),
                dma((2,)),
                dma((2,)),
                dma((2, 3)),
                dma((2, 3)),
                dma((3, gy)),
                dma((3, gy)),
                dma((2, 3)),
                dma((2, 3)),
                dma((gy,)),
                dma((gy,)),
                dma((sh.slabs + 1,)),
                dma((2, max(gx, gy))),
                dma((gy,)),
                dma((gx,)),
            ],
            compiler_params=pltpu.CompilerParams(
                collective_id=0, has_side_effects=True, vmem_limit_bytes=62_000_000
            ),
            name="interface_sweeps",
        )(fine_start, fine_known, fine_mu, coarse_start, coarse_known, coarse_mu)

    return jax.shard_map(
        on_device,
        mesh=mesh,
        in_specs=(
            P(None, "gx", "gy"),
            P(None, "gx", "gy"),
            P("gx", "gy"),
            P(None, ("gx", "gy"), None),
            P(None, ("gx", "gy"), None),
            P(("gx", "gy"), None),
        ),
        out_specs=(P(None, "gx", "gy"), P(None, ("gx", "gy"), None), P(None)),
        check_vma=False,
    )
```

profile of v0, /device:TPU:1, one launch (start us, length us, event | category | flops | bytes accessed | tf_op | source)
XLA Modules:
  0.0 65.1 jit_solution(1921061643503472922)
XLA Ops:
  0.6 60.5 %interface_sweeps.1 = (f32[3,256,512]{2,1,0:T(8,128)}, f32[3,8,4096]{2,1,0:T(8,128)}, f32[3]{0:T(128)}) custom-call(f32[3,256,512]{2,1,0:T(8,128)} %fine_start.1, f32[3,256,512]{2,1,0:T(8,128)} %fine_known.1, f32[256,512]{1,0:T(8,128)} %fine_mu.1, f32[3,8,4096]{2,1,0:T(8,128)} %coarse_start.1, f32[3,8,4096]{2,1,0:T(8,128)} %coarse_known.1, f32[8,4096]{1,0:T(8,128)} %coarse_mu.1), custom_call_target="tpu_custom_call" | custom-call | tf_op jit(solution)/shard_map/interface_sweeps/pallas_call | solution.py:736
  61.1 0.0 copy-start
  61.1 0.0 copy-start.1
  61.1 2.7 %copy.12 = f32[3,256,512]{2,1,0:T(8,128)} copy(f32[3,256,512]{2,1,0:T(8,128)} %get-tuple-element.6) | data formatting | bytes 3145728
  63.9 0.0 copy-done
  63.9 0.7 %copy.13 = f32[3,8,4096]{2,1,0:T(8,128)} copy(f32[3,8,4096]{2,1,0:T(8,128)S(1)} %copy-done) | data formatting | bytes 786432
  64.6 0.0 copy-done.1
  64.6 0.5 copy.14
Async XLA Ops:
  61.1 2.7 %copy-start = (f32[3,8,4096]{2,1,0:T(8,128)S(1)}, f32[3,8,4096]{2,1,0:T(8,128)}, u32[]{:S(2)}) copy-start(f32[3,8,4096]{2,1,0:T(8,128)} %get-tuple-element.7) | copy-start | bytes 1179652
  61.1 3.5 %copy-start.1 = (f32[3]{0:T(128)S(1)}, f32[3]{0:T(128)}, u32[]{:S(2)}) copy-start(f32[3]{0:T(128)} %get-tuple-element.8) | copy-start | bytes 40
where the time goes:
time: 65.3 us; the launch traced here: 65.1 us
  Pallas kernels  60.5 us (93%)
  local copies, waits for them, and re-layouts  3.98 us (6%)
  between operations  0.66 us (1%)
    pallas_call x1, Pallas kernels, on_device(): pl.pallas_call(functools.partial(kernel, sh), out_shape=(jax.ShapeDtypeSt...  60.5 us
    unnamed x7, local copies, waits for them, and re-layouts  3.98 us

commit v1 on v0

v1 whole, which is shorter than its diff:
```python
import functools

import jax
import jax.numpy as jnp
from jax import lax
from jax.experimental import pallas as pl
from jax.experimental.pallas import tpu as pltpu
from jax.sharding import PartitionSpec as P

MESH = pl.DeviceIdType.MESH
F32 = jnp.float32
BF16 = jnp.bfloat16
SWEEPS = 3
LANES = 128
SUB = 8
FINE_OFF = 24
COARSE_OFF = 16
EDGE = 4
PLANES = 7


class Shape:
    def __init__(self, gx, gy, fine_rows, fine_cols):
        self.gx, self.gy = gx, gy
        self.fine_rows, self.fine_cols = fine_rows, fine_cols
        self.coarse_rows, self.wide = fine_rows // 2, fine_cols // 2
        self.tiles = self.coarse_rows // SUB
        self.halves = self.wide // LANES
        self.slabs = 2 * self.halves
        self.fine_buf = fine_rows + 2 * FINE_OFF
        self.coarse_buf = self.coarse_rows + 2 * COARSE_OFF
        self.blocks = fine_rows // LANES
        self.cells = 3.0 * gx * gy * fine_rows * fine_cols * 1.25


def lane_iota():
    return lax.broadcasted_iota(jnp.int32, (SUB, LANES), 1)


def exact_dot(values, table):
    high = values.astype(BF16)
    rest = values - high.astype(F32)
    middle = rest.astype(BF16)
    low = (rest - middle.astype(F32)).astype(BF16)
    total = jnp.dot(high, table, preferred_element_type=F32)
    total = total + jnp.dot(middle, table, preferred_element_type=F32)
    return total + jnp.dot(low, table, preferred_element_type=F32)


def kernel(
    sh,
    fine_start,
    fine_known,
    fine_mu,
    coarse_start,
    coarse_known,
    coarse_mu,
    fine_out,
    coarse_out,
    norm_out,
    nat,
    turned,
    swapped,
    f_a,
    f_b,
    fd,
    fi,
    c_a,
    c_b,
    q_a,
    q_b,
    w_a,
    w_b,
    ckh,
    cd,
    ci,
    pre,
    own,
    comb,
    pack,
    got_c,
    got_p,
    got_k,
    edge_out,
    edge_in,
    fin,
    part,
    part_gy,
    part_gx,
    load_sem,
    edge_send,
    edge_recv,
    row_send,
    row_recv,
    a_send,
    a_recv,
    fwd_send,
    fwd_recv,
    fin_send,
    fin_recv,
    norm_send,
    norm_recv_y,
    norm_recv_x,
):
    gx, gy = sh.gx, sh.gy
    i = lax.axis_index("gx")
    j = lax.axis_index("gy")
    halves, slabs, tiles, wide = sh.halves, sh.slabs, sh.tiles, sh.wide
    halo, coarse_halo = slabs, halves
    lane = lane_iota()
    even = lane % 2 == 0
    first = lane == 0
    last = lane == LANES - 1
    has_up, has_down = i > 0, i < gx - 1
    has_left, has_right = j > 0, j < gy - 1

    def remote(src, dst, send, recv, to_i, to_j):
        return pltpu.make_async_remote_copy(
            src_ref=src,
            dst_ref=dst,
            send_sem=send,
            recv_sem=recv,
            device_id=(to_i, to_j),
            device_id_type=MESH,
        )

    loads = []

    def load(src, dst):
        copy = pltpu.make_async_copy(src, dst, load_sem.at[len(loads)])
        copy.start()
        loads.append(copy)
        return copy

    own_loads = [
        load(coarse_start, own.at[pl.ds(0, 3)]),
        load(coarse_known, own.at[pl.ds(3, 3)]),
        load(coarse_mu, own.at[6]),
    ]
    fine_loads = []
    for t in [0, slabs - 1] + list(range(1, slabs - 1)):
        cols = pl.ds(LANES * t, LANES)
        fine_loads.append(load(fine_start.at[:, :, cols], nat.at[pl.ds(0, 3), t]))
        fine_loads.append(load(fine_known.at[:, :, cols], nat.at[pl.ds(3, 3), t]))
        fine_loads.append(load(fine_mu.at[:, cols], nat.at[6, t]))

    zero = jnp.zeros((SUB, LANES), F32)
    fine_end = FINE_OFF + sh.fine_rows

    def zero_fine(step, carry):
        for row in (0, 8, 16, fine_end, fine_end + 8, fine_end + 16):
            rows = pl.ds(row, SUB)
            for p in range(PLANES):
                f_a[p, step, rows, :] = zero
            for k in range(3):
                f_b[k, step, rows, :] = zero
        for row in (0, 8, sh.coarse_buf - 16, sh.coarse_buf - 8):
            rows = pl.ds(row, SUB)
            for k in range(3):
                q_a[k, step, rows, :] = zero
                q_b[k, step, rows, :] = zero
        return carry

    lax.fori_loop(0, slabs + 1, zero_fine, 0)
    for t in range(halves + 1):
        for row in (0, 8, sh.coarse_buf - 16, sh.coarse_buf - 8):
            rows = pl.ds(row, SUB)
            for k in range(3):
                c_a[k, t, rows, :] = zero
                c_b[k, t, rows, :] = zero
    for side in range(2):
        for p in range(PLANES):
            edge_in[side, p] = zero
    for slot in (0, gy + 1):
        got_p[slot] = zero
        for u in range(halves):
            cols = pl.ds(LANES * u, LANES)
            for p in range(3):
                got_c[slot, p, :, cols] = zero
            for p in range(4):
                got_k[slot, p, :, cols] = zero

    barrier = pltpu.get_barrier_semaphore()
    for step in range(1, gy):
        pl.semaphore_signal(
            barrier, inc=1, device_id=(i, lax.rem(j + step, gy)), device_id_type=MESH
        )
    for step in range(1, gx):
        pl.semaphore_signal(
            barrier, inc=1, device_id=(lax.rem(i + step, gx), j), device_id_type=MESH
        )

    for copy in own_loads:
        copy.wait()

    for dest in range(gy):
        for p in range(PLANES):
            after = own[p, :, pl.ds((dest + 1) * wide, LANES)] if dest < gy - 1 else zero
            before = own[p, :, pl.ds(dest * wide - LANES, LANES)] if dest > 0 else zero
            comb[p, pl.ds(SUB * dest, SUB), :] = jnp.where(lane < 64, after, before)
    source = lax.broadcasted_iota(jnp.int32, (LANES, LANES), 0)
    target = lax.broadcasted_iota(jnp.int32, (LANES, LANES), 1)
    inside = target % 16
    wanted = jnp.where(inside < 8, LANES - EDGE + inside // 2, (inside - 8) // 2)
    packed = None
    for p in range(PLANES):
        table = ((source == wanted) & (target // 16 == p)).astype(F32).astype(BF16)
        piece = exact_dot(comb[p], table)
        packed = piece if packed is None else packed + piece
    for dest in range(gy):
        pack[dest] = packed[SUB * dest : SUB * (dest + 1), :]

    for copy in fine_loads:
        copy.wait()

    def turn_edges(p, carry):
        for b in range(sh.blocks):
            rows = pl.ds(LANES * b, LANES)
            low = nat[p, 0, rows, :].T
            high = nat[p, slabs - 1, rows, :].T
            turned[p, b, pl.ds(0, LANES), :] = low
            turned[p, b, pl.ds(LANES * (slabs - 1), LANES), :] = high
            edge_out[0, p, pl.ds(EDGE * b, EDGE), :] = high[LANES - EDGE :, :]
            edge_out[1, p, pl.ds(EDGE * b, EDGE), :] = low[:EDGE, :]
        return carry

    lax.fori_loop(0, PLANES, turn_edges, 0, unroll=PLANES)

    pl.semaphore_wait(barrier, gy + gx - 2)

    edge_right = remote(
        edge_out.at[0], edge_in.at[0], edge_send.at[0], edge_recv.at[0], i, lax.rem(j + 1, gy)
    )
    edge_left = remote(
        edge_out.at[1], edge_in.at[1], edge_send.at[1], edge_recv.at[1], i, lax.rem(j + gy - 1, gy)
    )

    @pl.when(has_right)
    def _():
        edge_right.start()

    @pl.when(has_left)
    def _():
        edge_left.start()

    def sends_of(step):
        to = lax.rem(j + step, gy)
        cols = pl.ds(pl.multiple_of(to * wide, LANES), wide)
        ends = (
            (own.at[pl.ds(0, 3), :, cols], got_c),
            (pack.at[to], got_p),
            (own.at[pl.ds(3, 4), :, cols], got_k),
        )
        return [
            remote(src, dst.at[j + 1], a_send.at[n, step], a_recv.at[n, step], i, to)
            for n, (src, dst) in enumerate(ends)
        ]

    order = list(range(1, gy))
    sends = {step: sends_of(step) for step in order}
    for step in order:
        sends[step][0].start()
        sends[step][1].start()
    for step in order:
        sends[step][2].start()

    got_p[j + 1] = pack[j]
    for u in range(halves):
        cols = pl.ds(pl.multiple_of(j * wide + LANES * u, LANES), LANES)
        for p in range(PLANES):
            piece = own[p, :, cols]
            if p < 3:
                got_c[j + 1, p, :, pl.ds(LANES * u, LANES)] = piece
            else:
                got_k[j + 1, p - 3, :, pl.ds(LANES * u, LANES)] = piece

    def split_columns(p, carry):
        for b in range(sh.blocks):
            rows = pl.ds(LANES * b, LANES)
            for t in range(1, slabs - 1):
                turned[p, b, pl.ds(LANES * t, LANES), :] = nat[p, t, rows, :].T
        for b in range(sh.blocks):
            rows = pl.ds(FINE_OFF + LANES * b, LANES)
            for s in range(slabs):
                begin = 2 * LANES * (s // 2) + s % 2
                f_a[p, s, rows, :] = turned[p, b, pl.ds(begin, LANES, stride=2), :].T
        return carry

    lax.fori_loop(0, PLANES, split_columns, 0)

    @pl.when(has_left)
    def _():
        edge_right.wait_recv()

    @pl.when(has_right)
    def _():
        edge_left.wait_recv()

    between = jnp.zeros((LANES - 2 * EDGE, LANES), F32)

    def unpack_edges(p, carry):
        for b in range(sh.blocks):
            from_left = edge_in[0, p, pl.ds(EDGE * b, EDGE), :]
            from_right = edge_in[1, p, pl.ds(EDGE * b, EDGE), :]
            slab = jnp.concatenate([from_right, between, from_left], axis=0).T
            f_a[p, halo, pl.ds(FINE_OFF + LANES * b, LANES), :] = slab
        return carry

    lax.fori_loop(0, PLANES, unpack_edges, 0, unroll=PLANES)

    down_i, up_i = lax.rem(i + 1, gx), lax.rem(i + gx - 1, gx)
    row_down = remote(
        f_a.at[:, :, pl.ds(fine_end - SUB, SUB), :],
        f_a.at[:, :, pl.ds(FINE_OFF - SUB, SUB), :],
        row_send.at[0],
        row_recv.at[0],
        down_i,
        j,
    )
    row_up = remote(
        f_a.at[:, :, pl.ds(FINE_OFF, SUB), :],
        f_a.at[:, :, pl.ds(fine_end, SUB), :],
        row_send.at[1],
        row_recv.at[1],
        up_i,
        j,
    )

    @pl.when(has_down)
    def _():
        row_down.start()

    @pl.when(has_up)
    def _():
        row_up.start()

    def coarse_row(m):
        return pl.multiple_of(COARSE_OFF + SUB * m, SUB)

    def halo_of(slot, p):
        return pltpu.roll(got_p[slot], (LANES - (16 * p + 8)) % LANES, 1)

    def swapped_pairs(value):
        return jnp.where(even, pltpu.roll(value, LANES - 1, 1), pltpu.roll(value, 1, 1))

    def produce(k, row, values, c_ref, q_ref, w_ref):
        right = [pltpu.roll(v, 1, 1) for v in values]
        left = [pltpu.roll(v, LANES - 1, 1) for v in values]
        rows = pl.ds(row, SUB)
        count = len(values)
        for t, value in enumerate(values):
            before = jnp.where(first, right[t - 1], right[t])
            after = jnp.where(last, left[(t + 1) % count], left[t])
            c_ref[k, t, rows, :] = value
            main = 0.375 * value
            if t == coarse_halo:
                outer = jnp.where(even, before, after)
                q_ref[k, halo, rows, :] = main + 0.125 * outer
                w_ref[k, t, rows, :] = outer + swapped_pairs(outer)
            else:
                q_ref[k, 2 * t, rows, :] = main + 0.125 * before
                q_ref[k, 2 * t + 1, rows, :] = main + 0.125 * after
                w_ref[k, t, rows, :] = before + after

    def spread_first(slot, carry):
        for k in range(3):
            values = [got_c[slot, k, :, pl.ds(LANES * t, LANES)] for t in range(halves)]
            values.append(halo_of(slot, k))
            produce(k, coarse_row(slot - 1), values, c_a, q_a, w_a)
        return carry

    halo_lanes = ((lane < 2 * EDGE) & has_right) | ((lane >= LANES - 2 * EDGE) & has_left)
    halo_lanes_fine = ((lane < EDGE) & has_right) | ((lane >= LANES - EDGE) & has_left)

    def spread_second(slot, carry):
        rows = pl.ds(coarse_row(slot - 1), SUB)
        held = ((slot > 0) | has_up) & ((slot <= gy) | has_down)
        for k in range(3):
            ckh[k, rows, :] = halo_of(slot, 3 + k)
        for t in range(halves + 1):
            if t == coarse_halo:
                value, valid = halo_of(slot, 6), halo_lanes & held
            else:
                value, valid = got_k[slot, 3, :, pl.ds(LANES * t, LANES)], (lane >= 0) & held
            diag = value + 1.0
            cd[t, rows, :] = diag
            ci[t, rows, :] = jnp.where(valid, 1.0 / diag, 0.0)
        return carry

    fwd_copies = {}
    for n, ref in enumerate((got_c, got_p, got_k)):
        fwd_copies[n] = (
            remote(ref.at[gy], ref.at[0], fwd_send.at[0, n], fwd_recv.at[0, n], down_i, j),
            remote(ref.at[1], ref.at[gy + 1], fwd_send.at[1, n], fwd_recv.at[1, n], up_i, j),
        )

    def wait_from(kinds, source):
        step = lax.rem(j - source + gy, gy)

        @pl.when(step > 0)
        def _():
            for kind in kinds:
                dst = (got_c, got_p, got_k)[kind].at[source + 1]
                remote(dst, dst, a_send.at[kind, step], a_recv.at[kind, step], i, source).wait_recv()

    def pass_on(kinds):
        wait_from(kinds, gy - 1)

        @pl.when(has_down)
        def _():
            for kind in kinds:
                fwd_copies[kind][0].start()

        wait_from(kinds, 0)

        @pl.when(has_up)
        def _():
            for kind in kinds:
                fwd_copies[kind][1].start()

        def rest(source, carry):
            wait_from(kinds, source)
            return carry

        lax.fori_loop(1, gy - 1, rest, 0)

    def passed_on(kinds):
        @pl.when(has_up)
        def _():
            for kind in kinds:
                fwd_copies[kind][0].wait_recv()

        @pl.when(has_down)
        def _():
            for kind in kinds:
                fwd_copies[kind][1].wait_recv()

    def diagonal(row, held):
        rows = pl.ds(row, SUB)
        for t in range(slabs + 1):
            diag = f_a[6, t, rows, :] + 1.0
            valid = (halo_lanes_fine if t == halo else (lane >= 0)) & held
            fd[t, rows, :] = diag
            fi[t, rows, :] = jnp.where(valid, 1.0 / diag, 0.0)

    def diagonals(step, carry):
        for n in range(4):
            diagonal(pl.multiple_of(FINE_OFF + SUB * (4 * step + n), SUB), lane >= 0)
        return carry

    lax.fori_loop(0, sh.fine_rows // (4 * SUB), diagonals, 0)

    pass_on((0, 1))
    lax.fori_loop(1, gy + 1, spread_first, 0, unroll=8)

    @pl.when(has_up)
    def _():
        row_down.wait_recv()

    @pl.when(has_down)
    def _():
        row_up.wait_recv()

    for row, held in (
        (FINE_OFF - 16, lane < 0),
        (FINE_OFF - 8, (lane >= 0) & has_up),
        (fine_end, (lane >= 0) & has_down),
        (fine_end + 8, lane < 0),
    ):
        diagonal(row, held)

    passed_on((0, 1))
    lax.fori_loop(0, 2, lambda e, c: spread_first((gy + 1) * e, c), 0, unroll=2)

    def beside(values):
        side = values[halo]
        odd_right = [pltpu.roll(values[2 * h + 1], 1, 1) for h in range(halves)]
        even_left = [pltpu.roll(values[2 * h], LANES - 1, 1) for h in range(halves)]
        side_right, side_left = pltpu.roll(side, 1, 1), pltpu.roll(side, LANES - 1, 1)
        sums = []
        for h in range(halves):
            before = odd_right[h - 1] if h > 0 else side_right
            after = even_left[h + 1] if h < halves - 1 else side_left
            sums.append(jnp.where(first, before, odd_right[h]) + values[2 * h + 1])
            sums.append(values[2 * h] + jnp.where(last, after, even_left[h]))
        sums.append(
            jnp.where(first, odd_right[-1], side_right) + jnp.where(last, even_left[0], side_left)
        )
        return sums

    def fine_tile(m, acc, f_in, q_ref, f_out, count):
        base = FINE_OFF + 16 * m
        upper, lower = pl.ds(base, SUB, stride=2), pl.ds(base + 1, SUB, stride=2)
        above, below = pl.ds(base - 1, SUB, stride=2), pl.ds(base + 2, SUB, stride=2)
        crow = COARSE_OFF + SUB * m
        q_here, q_up, q_down = pl.ds(crow, SUB), pl.ds(crow - 1, SUB), pl.ds(crow + 1, SUB)
        for k in range(3):
            tops = [f_in[k, t, upper, :] for t in range(slabs + 1)]
            lows = [f_in[k, t, lower, :] for t in range(slabs + 1)]
            top_sum, low_sum = beside(tops), beside(lows)
            for t in range(count):
                three = 3.0 * q_ref[k, t, q_here, :]
                nb = (lows[t] + f_in[k, t, above, :]) + (top_sum[t] + q_ref[k, t, q_up, :])
                total = f_a[3 + k, t, upper, :] + 0.25 * (nb + three)
                res = total - fd[t, upper, :] * tops[t]
                f_out[k, t, upper, :] = total * fi[t, upper, :]
                nb2 = (tops[t] + f_in[k, t, below, :]) + (low_sum[t] + q_ref[k, t, q_down, :])
                total2 = f_a[3 + k, t, lower, :] + 0.25 * (nb2 + three)
                res2 = total2 - fd[t, lower, :] * lows[t]
                f_out[k, t, lower, :] = total2 * fi[t, lower, :]
                if acc is not None and t < slabs:
                    acc = acc + (res * res + res2 * res2)
        return acc

    def coarse_sum(m, k, t, f_in, c_ref, w_ref):
        base = FINE_OFF + 16 * m
        crow = COARSE_OFF + SUB * m
        upper, lower = pl.ds(base, SUB, stride=2), pl.ds(base + 1, SUB, stride=2)
        if t == coarse_halo:
            four = f_in[k, halo, upper, :] + f_in[k, halo, lower, :]
            four = four + swapped_pairs(four)
        else:
            four = (f_in[k, 2 * t, upper, :] + f_in[k, 2 * t, lower, :]) + (
                f_in[k, 2 * t + 1, upper, :] + f_in[k, 2 * t + 1, lower, :]
            )
        nb = c_ref[k, t, pl.ds(crow - 1, SUB), :] + c_ref[k, t, pl.ds(crow + 1, SUB), :]
        nb = nb + w_ref[k, t, pl.ds(coarse_row(m), SUB), :]
        return 0.25 * (nb + 0.5 * four)

    def coarse_step(m, k, t, acc, added, c_ref):
        rows = pl.ds(coarse_row(m), SUB)
        if t == coarse_halo:
            known = ckh[k, rows, :]
        else:
            known = got_k[m + 1, k, :, pl.ds(LANES * t, LANES)]
        total = known + added
        if acc is not None and t < halves:
            res = total - cd[t, rows, :] * c_ref[k, t, rows, :]
            acc = acc + res * res
        return total * ci[t, rows, :], acc

    def first_sum(m, carry):
        rows = pl.ds(coarse_row(m), SUB)
        for k in range(3):
            for t in range(halves + 1):
                pre[k, t, rows, :] = coarse_sum(m, k, t, f_a, c_a, w_a)
        return zero

    def first_coarse(m, acc):
        rows = pl.ds(coarse_row(m), SUB)
        for k in range(3):
            values = []
            for t in range(halves + 1):
                value, acc = coarse_step(m, k, t, acc, pre[k, t, rows, :], c_a)
                values.append(value)
            produce(k, coarse_row(m), values, c_b, q_b, w_b)
        return acc

    def second_coarse(m, acc):
        for k in range(3):
            values = []
            for t in range(halves + 1):
                added = coarse_sum(m, k, t, f_b, c_b, w_b)
                value, acc = coarse_step(m, k, t, acc, added, c_b)
                values.append(value)
            produce(k, coarse_row(m), values, c_a, q_a, w_a)
        return acc

    def third_coarse(m, acc):
        for k in range(3):
            for t in range(halves):
                added = coarse_sum(m, k, t, f_a, c_a, w_a)
                value, acc = coarse_step(m, k, t, acc, added, c_a)
                fin[m, k, :, pl.ds(LANES * t, LANES)] = value
        return acc

    def every_tile(body, acc, unroll=6):
        def step(n, acc):
            m = n - 1
            part_sum = body(m, zero)
            inner = jnp.where((n > 0) & (n <= tiles), 1.0, 0.0).astype(F32)
            return acc + part_sum * inner

        return lax.fori_loop(0, tiles + 2, step, acc, unroll=unroll)

    def fine_first(m, acc):
        return fine_tile(m, acc, f_a, q_a, f_b, slabs + 1)

    def fine_second(m, acc):
        return fine_tile(m, acc, f_b, q_b, f_a, slabs + 1)

    def fine_third(m, acc):
        return fine_tile(m, acc, f_a, q_a, f_b, slabs)

    fine_sum1 = every_tile(fine_first, zero)
    every_tile(first_sum, zero)

    pass_on((2,))
    lax.fori_loop(1, gy + 1, spread_second, 0, unroll=8)
    passed_on((2,))
    lax.fori_loop(0, 2, lambda e, c: spread_second((gy + 1) * e, c), 0, unroll=2)

    coarse_sum1 = every_tile(first_coarse, zero)

    @pl.when(has_down)
    def _():
        row_down.wait_send()

    @pl.when(has_up)
    def _():
        row_up.wait_send()

    fine_sum2 = every_tile(fine_second, zero)
    coarse_sum2 = every_tile(second_coarse, zero)
    coarse_sum3 = lax.fori_loop(0, tiles, third_coarse, zero, unroll=4)

    my_cols = pl.ds(pl.multiple_of(j * wide, LANES), wide)
    finals = []
    for step in order:
        to = lax.rem(j + step, gy)
        copy = remote(
            fin.at[to], coarse_out.at[:, :, my_cols], fin_send.at[step], fin_recv.at[step], i, to
        )
        copy.start()
        finals.append(copy)
    for k in range(3):
        for t in range(halves):
            cols = pl.ds(pl.multiple_of(j * wide + LANES * t, LANES), LANES)
            coarse_out[k, :, cols] = fin[j, k, :, pl.ds(LANES * t, LANES)]

    fine_sum3 = lax.fori_loop(0, tiles, fine_third, zero, unroll=8)

    row_of = lax.broadcasted_iota(jnp.int32, (SUB, LANES), 0)
    mine = zero
    sums = ((fine_sum1, coarse_sum1), (fine_sum2, coarse_sum2), (fine_sum3, coarse_sum3))
    for s, (fine_part, coarse_part) in enumerate(sums):
        line = jnp.sum(fine_part + coarse_part, axis=0, keepdims=True)
        mine = jnp.where(row_of == s, line, mine)
    part[0] = mine
    norm_x = []
    for step in range(1, gx):
        copy = remote(
            part.at[0],
            part_gx.at[step],
            norm_send.at[0, step],
            norm_recv_x.at[step],
            lax.rem(i + step, gx),
            j,
        )
        copy.start()
        norm_x.append(copy)

    def join_columns(k, carry):
        for b in range(sh.blocks):
            rows = pl.ds(FINE_OFF + LANES * b, LANES)
            for s in range(slabs):
                begin = 2 * LANES * (s // 2) + s % 2
                swapped[b, pl.ds(begin, LANES, stride=2), :] = f_b[k, s, rows, :].T
            for t in range(slabs):
                natural = swapped[b, pl.ds(LANES * t, LANES), :].T
                fine_out[k, pl.ds(LANES * b, LANES), pl.ds(LANES * t, LANES)] = natural
        return carry

    lax.fori_loop(0, 3, join_columns, 0)

    for copy in norm_x:
        copy.wait_recv()
    for step in range(1, gx):
        mine = mine + part_gx[step]
    part[1] = mine
    norm_y = []
    for step in order:
        copy = remote(
            part.at[1],
            part_gy.at[step],
            norm_send.at[1, step],
            norm_recv_y.at[step],
            i,
            lax.rem(j + step, gy),
        )
        copy.start()
        norm_y.append(copy)
    for copy in norm_y:
        copy.wait_recv()
    for step in order:
        mine = mine + part_gy[step]
    total = jnp.sum(mine, axis=1, keepdims=True) * (1.0 / sh.cells)
    norms = jnp.sqrt(total)
    for s in range(SWEEPS):
        norm_out[s] = norms[s, 0]

    @pl.when(has_right)
    def _():
        edge_right.wait_send()

    @pl.when(has_left)
    def _():
        edge_left.wait_send()

    @pl.when(has_down)
    def _():
        for kind in range(3):
            fwd_copies[kind][0].wait_send()

    @pl.when(has_up)
    def _():
        for kind in range(3):
            fwd_copies[kind][1].wait_send()

    for step in order:
        for copy in sends[step]:
            copy.wait_send()
    for copy in finals:
        copy.wait()
    for copy in norm_y + norm_x:
        copy.wait_send()


def solution(mesh):
    gx, gy = mesh.shape["gx"], mesh.shape["gy"]

    def on_device(fine_start, fine_known, fine_mu, coarse_start, coarse_known, coarse_mu):
        sh = Shape(gx, gy, *fine_mu.shape)
        dma = pltpu.SemaphoreType.DMA
        in_hbm = pl.BlockSpec(memory_space=pltpu.HBM)
        on_chip = pl.BlockSpec(memory_space=pltpu.VMEM)

        def fine(*lead):
            return pltpu.VMEM((*lead, sh.slabs + 1, sh.fine_buf, LANES), F32)

        def coarse(*lead):
            return pltpu.VMEM((*lead, sh.coarse_buf, LANES), F32)

        few = sh.halves + 1
        return pl.pallas_call(
            functools.partial(kernel, sh),
            out_shape=(
                pltpu.VMEM(fine_start.shape, F32),
                pltpu.VMEM(coarse_start.shape, F32),
                jax.ShapeDtypeStruct((SWEEPS,), F32),
            ),
            in_specs=[in_hbm] * 6,
            out_specs=(on_chip, on_chip, pl.BlockSpec(memory_space=pltpu.SMEM)),
            scratch_shapes=[
                pltpu.VMEM((PLANES, sh.slabs, sh.fine_rows, LANES), F32),
                pltpu.VMEM((PLANES, sh.blocks, sh.slabs * LANES, LANES), F32),
                pltpu.VMEM((sh.blocks, sh.slabs * LANES, LANES), F32),
                fine(PLANES),
                fine(3),
                fine(),
                fine(),
                coarse(3, few),
                coarse(3, few),
                coarse(3, sh.slabs + 1),
                coarse(3, sh.slabs + 1),
                coarse(3, few),
                coarse(3, few),
                coarse(3),
                coarse(few),
                coarse(few),
                coarse(3, few),
                pltpu.VMEM((PLANES, SUB, gy * sh.wide), F32),
                pltpu.VMEM((PLANES, gy * SUB, LANES), F32),
                pltpu.VMEM((gy, SUB, LANES), F32),
                pltpu.VMEM((gy + 2, 3, SUB, sh.wide), F32),
                pltpu.VMEM((gy + 2, SUB, LANES), F32),
                pltpu.VMEM((gy + 2, 4, SUB, sh.wide), F32),
                pltpu.VMEM((2, PLANES, SUB, LANES), F32),
                pltpu.VMEM((2, PLANES, SUB, LANES), F32),
                pltpu.VMEM((gy, 3, SUB, sh.wide), F32),
                pltpu.VMEM((2, SUB, LANES), F32),
                pltpu.VMEM((gy, SUB, LANES), F32),
                pltpu.VMEM((gx, SUB, LANES), F32),
                dma((3 + 3 * sh.slabs,)),
                dma((2,)),
                dma((2,)),
                dma((2,)),
                dma((2,)),
                dma((3, gy)),
                dma((3, gy)),
                dma((2, 3)),
                dma((2, 3)),
                dma((gy,)),
                dma((gy,)),
                dma((2, max(gx, gy))),
                dma((gy,)),
                dma((gx,)),
            ],
            compiler_params=pltpu.CompilerParams(
                collective_id=0, has_side_effects=True, vmem_limit_bytes=64_500_000
            ),
            name="interface_sweeps",
        )(fine_start, fine_known, fine_mu, coarse_start, coarse_known, coarse_mu)

    return jax.shard_map(
        on_device,
        mesh=mesh,
        in_specs=(
            P(None, "gx", "gy"),
            P(None, "gx", "gy"),
            P("gx", "gy"),
            P(None, ("gx", "gy"), None),
            P(None, ("gx", "gy"), None),
            P(("gx", "gy"), None),
        ),
        out_specs=(P(None, "gx", "gy"), P(None, ("gx", "gy"), None), P(None)),
        check_vma=False,
    )
```

time: 65.3 us -> 46.5 us (0.71)
  Pallas kernels: 60.5 us -> 43.3 us
  local copies, waits for them, and re-layouts: 3.98 us -> 2.41 us
    pallas_call x1, Pallas kernels: 60.5 us -> 43.3 us  [on_device(): pl.pallas_call(functools.partial(kernel, sh), out_shape=(pltpu.VMEM(fine_...]
    unnamed x7 -> x5, local copies, waits for them, and re-layouts: 3.98 us -> 2.41 us
where the time goes in v1:
time: 46.5 us; the launch traced here: 46.3 us
  Pallas kernels  43.3 us (93%)
  local copies, waits for them, and re-layouts  2.41 us (5%)
  between operations  0.65 us (1%)
    pallas_call x1, Pallas kernels, on_device(): pl.pallas_call(functools.partial(kernel, sh), out_shape=(pltpu.VMEM(fine_...  43.3 us
    unnamed x5, local copies, waits for them, and re-layouts  2.41 us

profile of v1, /device:TPU:1, one launch (start us, length us, event | category | flops | bytes accessed | tf_op | source)
XLA Modules:
  0.0 46.3 jit_solution(15206673814427907202)
XLA Ops:
  0.6 43.3 %interface_sweeps.1 = (f32[3,256,512]{2,1,0:T(8,128)S(1)}, f32[3,8,4096]{2,1,0:T(8,128)S(1)}, f32[3]{0:T(128)}) custom-call(f32[3,256,512]{2,1,0:T(8,128)} %fine_start.1, f32[3,256,512]{2,1,0:T(8,128)} %fine_known.1, f32[256,512]{1,0:T(8,128)} %fine_mu.1, f32[3,8,4096]{2,1,0:T(8,128)} %coarse_start.1, f32[3,8,4096]{2,1,0:T(8,128)} %coarse_known.1, ...), custom_call_target="tpu_custom_call" | custom-call | tf_op jit(solution)/shard_map/interface_sweeps/pallas_call | solution.py:735
  43.9 0.0 copy-start
  43.9 1.1 %copy.12 = f32[3,256,512]{2,1,0:T(8,128)} copy(f32[3,256,512]{2,1,0:T(8,128)S(1)} %get-tuple-element.3) | data formatting | bytes 3145728
  45.1 0.7 %copy.13 = f32[3,8,4096]{2,1,0:T(8,128)} copy(f32[3,8,4096]{2,1,0:T(8,128)S(1)} %get-tuple-element.4) | data formatting | bytes 786432
  45.8 0.0 copy-done
  45.8 0.5 %copy.14 = f32[3]{0:T(128)} copy(f32[3]{0:T(128)S(1)} %copy-done) | data formatting | bytes 24
Async XLA Ops:
  43.9 1.9 %copy-start = (f32[3]{0:T(128)S(1)}, f32[3]{0:T(128)}, u32[]{:S(2)}) copy-start(f32[3]{0:T(128)} %get-tuple-element.11) | copy-start | bytes 40

commit v2 on v1

--- a/solution.py
+++ b/solution.py
@@ -28,9 +28,13 @@
         self.halves = self.wide // LANES
         self.slabs = 2 * self.halves
         self.fine_buf = fine_rows + 2 * FINE_OFF
-        self.coarse_buf = self.coarse_rows + 2 * COARSE_OFF
+        self.coarse_buf = self.coarse_rows + 2 * COARSE_OFF + SUB
         self.blocks = fine_rows // LANES
         self.cells = 3.0 * gx * gy * fine_rows * fine_cols * 1.25
+
+
+def far_first(count):
+    return sorted(range(1, count), key=lambda step: -min(step, count - step))
 
 
 def lane_iota():
@@ -75,12 +79,17 @@
     cd,
     ci,
     pre,
+    pre_b,
+    near,
     own,
     comb,
     pack,
     got_c,
     got_p,
     got_k,
+    strip_out,
+    strip_in,
+    strip_far,
     edge_out,
     edge_in,
     fin,
@@ -96,6 +105,8 @@
     a_recv,
     fwd_send,
     fwd_recv,
+    strip_send,
+    strip_recv,
     fin_send,
     fin_recv,
     norm_send,
@@ -144,51 +155,54 @@
         fine_loads.append(load(fine_known.at[:, :, cols], nat.at[pl.ds(3, 3), t]))
         fine_loads.append(load(fine_mu.at[:, cols], nat.at[6, t]))
 
-    zero = jnp.zeros((SUB, LANES), F32)
-    fine_end = FINE_OFF + sh.fine_rows
-
-    def zero_fine(step, carry):
-        for row in (0, 8, 16, fine_end, fine_end + 8, fine_end + 16):
-            rows = pl.ds(row, SUB)
-            for p in range(PLANES):
-                f_a[p, step, rows, :] = zero
-            for k in range(3):
-                f_b[k, step, rows, :] = zero
-        for row in (0, 8, sh.coarse_buf - 16, sh.coarse_buf - 8):
-            rows = pl.ds(row, SUB)
-            for k in range(3):
-                q_a[k, step, rows, :] = zero
-                q_b[k, step, rows, :] = zero
-        return carry
-
-    lax.fori_loop(0, slabs + 1, zero_fine, 0)
-    for t in range(halves + 1):
-        for row in (0, 8, sh.coarse_buf - 16, sh.coarse_buf - 8):
-            rows = pl.ds(row, SUB)
-            for k in range(3):
-                c_a[k, t, rows, :] = zero
-                c_b[k, t, rows, :] = zero
-    for side in range(2):
-        for p in range(PLANES):
-            edge_in[side, p] = zero
-    for slot in (0, gy + 1):
-        got_p[slot] = zero
-        for u in range(halves):
-            cols = pl.ds(LANES * u, LANES)
-            for p in range(3):
-                got_c[slot, p, :, cols] = zero
-            for p in range(4):
-                got_k[slot, p, :, cols] = zero
-
     barrier = pltpu.get_barrier_semaphore()
-    for step in range(1, gy):
+    for step in far_first(gy):
         pl.semaphore_signal(
             barrier, inc=1, device_id=(i, lax.rem(j + step, gy)), device_id_type=MESH
         )
-    for step in range(1, gx):
+    for step in far_first(gx):
         pl.semaphore_signal(
             barrier, inc=1, device_id=(lax.rem(i + step, gx), j), device_id_type=MESH
         )
+
+    zero = jnp.zeros((SUB, LANES), F32)
+    fine_end = FINE_OFF + sh.fine_rows
+    for t in range(slabs + 1):
+        for row in (0, 8, fine_end + 8, fine_end + 16):
+            for p in range(PLANES):
+                f_a[p, t, pl.ds(row, SUB), :] = zero
+        for k in range(3):
+            for row in (0, fine_end + 16):
+                f_b[k, t, pl.ds(row, SUB), :] = zero
+            for row in (0, sh.coarse_buf - 8):
+                q_a[k, t, pl.ds(row, SUB), :] = zero
+                q_b[k, t, pl.ds(row, SUB), :] = zero
+                if t <= halves:
+                    c_a[k, t, pl.ds(row, SUB), :] = zero
+                    c_b[k, t, pl.ds(row, SUB), :] = zero
+
+    for slot in (0, gy + 1):
+        for u in range(halves):
+            for p in range(4):
+                got_k[slot, p, :, pl.ds(LANES * u, LANES)] = zero
+
+    def clear_rows(row, slot):
+        for p in range(PLANES):
+            for t in range(slabs + 1):
+                f_a[p, t, pl.ds(row, SUB), :] = zero
+        got_p[slot] = zero
+        for u in range(halves):
+            for p in range(3):
+                got_c[slot, p, :, pl.ds(LANES * u, LANES)] = zero
+
+    def clear_columns(side):
+        for p in range(PLANES):
+            edge_in[side, p] = zero
+
+    pl.when(i == 0)(lambda: clear_rows(FINE_OFF - SUB, 0))
+    pl.when(i == gx - 1)(lambda: clear_rows(fine_end, gy + 1))
+    pl.when(j == 0)(lambda: clear_columns(0))
+    pl.when(j == gy - 1)(lambda: clear_columns(1))
 
     for copy in own_loads:
         copy.wait()
@@ -210,6 +224,15 @@
     for dest in range(gy):
         pack[dest] = packed[SUB * dest : SUB * (dest + 1), :]
 
+    def pack_strip(begin):
+        for dest in range(gy):
+            for p in range(4):
+                piece = own[3 + p, begin : begin + 2, pl.ds(dest * wide, wide)]
+                strip_out[dest, pl.ds(2 * p, 2), :] = piece
+
+    pl.when(j == gy - 1)(lambda: pack_strip(SUB - 2))
+    pl.when(j == 0)(lambda: pack_strip(0))
+
     for copy in fine_loads:
         copy.wait()
 
@@ -258,9 +281,23 @@
 
     order = list(range(1, gy))
     sends = {step: sends_of(step) for step in order}
+    def strip_of(step, side):
+        to = lax.rem(j + step, gy)
+        return remote(
+            strip_out.at[to], strip_in.at[side], strip_send.at[step], strip_recv.at[side], i, to
+        )
+
     for step in order:
         sends[step][0].start()
         sends[step][1].start()
+
+    def send_strips(side):
+        for step in order:
+            strip_of(step, side).start()
+        strip_in[side] = strip_out[j]
+
+    pl.when(j == gy - 1)(lambda: send_strips(0))
+    pl.when(j == 0)(lambda: send_strips(1))
     for step in order:
         sends[step][2].start()
 
@@ -388,11 +425,35 @@
         return carry
 
     fwd_copies = {}
-    for n, ref in enumerate((got_c, got_p, got_k)):
+    for n, ref in enumerate((got_c, got_p)):
         fwd_copies[n] = (
             remote(ref.at[gy], ref.at[0], fwd_send.at[0, n], fwd_recv.at[0, n], down_i, j),
             remote(ref.at[1], ref.at[gy + 1], fwd_send.at[1, n], fwd_recv.at[1, n], up_i, j),
         )
+
+    strip_copies = (
+        remote(strip_in.at[0], strip_far.at[0], fwd_send.at[0, 2], fwd_recv.at[0, 2], down_i, j),
+        remote(strip_in.at[1], strip_far.at[1], fwd_send.at[1, 2], fwd_recv.at[1, 2], up_i, j),
+    )
+
+    def pass_strips_on():
+        pl.when(j < gy - 1)(lambda: strip_of(1, 0).wait_recv())
+        pl.when(has_down)(lambda: strip_copies[0].start())
+        pl.when(j > 0)(lambda: strip_of(1, 1).wait_recv())
+        pl.when(has_up)(lambda: strip_copies[1].start())
+
+    def strips_passed_on():
+        @pl.when(has_up)
+        def _():
+            strip_copies[0].wait_recv()
+            for p in range(4):
+                got_k[0, p, pl.ds(SUB - 2, 2), :] = strip_far[0, pl.ds(2 * p, 2), :]
+
+        @pl.when(has_down)
+        def _():
+            strip_copies[1].wait_recv()
+            for p in range(4):
+                got_k[gy + 1, p, pl.ds(0, 2), :] = strip_far[1, pl.ds(2 * p, 2), :]
 
     def wait_from(kinds, source):
         step = lax.rem(j - source + gy, gy)
@@ -418,6 +479,7 @@
             for kind in kinds:
                 fwd_copies[kind][1].start()
 
+    def wait_rest(kinds):
         def rest(source, carry):
             wait_from(kinds, source)
             return carry
@@ -451,8 +513,10 @@
     lax.fori_loop(0, sh.fine_rows // (4 * SUB), diagonals, 0)
 
     pass_on((0, 1))
-    lax.fori_loop(1, gy + 1, spread_first, 0, unroll=8)
-
+    wait_rest((0, 1))
+    lax.fori_loop(1, gy + 1, spread_first, 0, unroll=4)
+
+    pass_strips_on()
     @pl.when(has_up)
     def _():
         row_down.wait_recv()
@@ -514,7 +578,6 @@
 
     def coarse_sum(m, k, t, f_in, c_ref, w_ref):
         base = FINE_OFF + 16 * m
-        crow = COARSE_OFF + SUB * m
         upper, lower = pl.ds(base, SUB, stride=2), pl.ds(base + 1, SUB, stride=2)
         if t == coarse_halo:
             four = f_in[k, halo, upper, :] + f_in[k, halo, lower, :]
@@ -523,9 +586,7 @@
             four = (f_in[k, 2 * t, upper, :] + f_in[k, 2 * t, lower, :]) + (
                 f_in[k, 2 * t + 1, upper, :] + f_in[k, 2 * t + 1, lower, :]
             )
-        nb = c_ref[k, t, pl.ds(crow - 1, SUB), :] + c_ref[k, t, pl.ds(crow + 1, SUB), :]
-        nb = nb + w_ref[k, t, pl.ds(coarse_row(m), SUB), :]
-        return 0.25 * (nb + 0.5 * four)
+        return 0.25 * (coarse_near(m, k, t, c_ref, w_ref) + 0.5 * four)
 
     def coarse_step(m, k, t, acc, added, c_ref):
         rows = pl.ds(coarse_row(m), SUB)
@@ -539,6 +600,50 @@
             acc = acc + res * res
         return total * ci[t, rows, :], acc
 
+    def near_sum(m, carry):
+        base = FINE_OFF + 16 * m
+        upper, lower = pl.ds(base, SUB, stride=2), pl.ds(base + 1, SUB, stride=2)
+        above, below = pl.ds(base - 1, SUB, stride=2), pl.ds(base + 2, SUB, stride=2)
+        for k in range(3):
+            tops = [f_b[k, t, upper, :] for t in range(slabs + 1)]
+            lows = [f_b[k, t, lower, :] for t in range(slabs + 1)]
+            top_sum, low_sum = beside(tops), beside(lows)
+            both = [tops[t] + lows[t] for t in range(slabs + 1)]
+            for t in range(slabs + 1):
+                nb = (lows[t] + f_b[k, t, above, :]) + top_sum[t]
+                near[k, t, upper, :] = f_a[3 + k, t, upper, :] + 0.25 * nb
+                nb2 = (tops[t] + f_b[k, t, below, :]) + low_sum[t]
+                near[k, t, lower, :] = f_a[3 + k, t, lower, :] + 0.25 * nb2
+            rows = pl.ds(coarse_row(m), SUB)
+            for t in range(halves):
+                pre_b[k, t, rows, :] = 0.125 * (both[2 * t] + both[2 * t + 1])
+            side = both[halo]
+            pre_b[k, coarse_halo, rows, :] = 0.125 * (side + swapped_pairs(side))
+        return zero
+
+    def second_fine(m, acc):
+        base = FINE_OFF + 16 * m
+        upper, lower = pl.ds(base, SUB, stride=2), pl.ds(base + 1, SUB, stride=2)
+        crow = COARSE_OFF + SUB * m
+        q_here, q_up, q_down = pl.ds(crow, SUB), pl.ds(crow - 1, SUB), pl.ds(crow + 1, SUB)
+        for k in range(3):
+            for t in range(slabs + 1):
+                three = 0.75 * q_b[k, t, q_here, :]
+                total = near[k, t, upper, :] + (three + 0.25 * q_b[k, t, q_up, :])
+                res = total - fd[t, upper, :] * f_b[k, t, upper, :]
+                f_a[k, t, upper, :] = total * fi[t, upper, :]
+                total2 = near[k, t, lower, :] + (three + 0.25 * q_b[k, t, q_down, :])
+                res2 = total2 - fd[t, lower, :] * f_b[k, t, lower, :]
+                f_a[k, t, lower, :] = total2 * fi[t, lower, :]
+                if t < slabs:
+                    acc = acc + (res * res + res2 * res2)
+        return acc
+
+    def coarse_near(m, k, t, c_ref, w_ref):
+        crow = COARSE_OFF + SUB * m
+        nb = c_ref[k, t, pl.ds(crow - 1, SUB), :] + c_ref[k, t, pl.ds(crow + 1, SUB), :]
+        return nb + w_ref[k, t, pl.ds(coarse_row(m), SUB), :]
+
     def first_sum(m, carry):
         rows = pl.ds(coarse_row(m), SUB)
         for k in range(3):
@@ -560,7 +665,8 @@
         for k in range(3):
             values = []
             for t in range(halves + 1):
-                added = coarse_sum(m, k, t, f_b, c_b, w_b)
+                added = pre_b[k, t, pl.ds(coarse_row(m), SUB), :]
+                added = added + 0.25 * coarse_near(m, k, t, c_b, w_b)
                 value, acc = coarse_step(m, k, t, acc, added, c_b)
                 values.append(value)
             produce(k, coarse_row(m), values, c_a, q_a, w_a)
@@ -586,21 +692,21 @@
     def fine_first(m, acc):
         return fine_tile(m, acc, f_a, q_a, f_b, slabs + 1)
 
-    def fine_second(m, acc):
-        return fine_tile(m, acc, f_b, q_b, f_a, slabs + 1)
-
     def fine_third(m, acc):
         return fine_tile(m, acc, f_a, q_a, f_b, slabs)
 
     fine_sum1 = every_tile(fine_first, zero)
     every_tile(first_sum, zero)
-
-    pass_on((2,))
+    every_tile(near_sum, zero)
+
+    wait_from((2,), 0)
+    wait_from((2,), gy - 1)
+    wait_rest((2,))
     lax.fori_loop(1, gy + 1, spread_second, 0, unroll=8)
-    passed_on((2,))
+    strips_passed_on()
     lax.fori_loop(0, 2, lambda e, c: spread_second((gy + 1) * e, c), 0, unroll=2)
 
-    coarse_sum1 = every_tile(first_coarse, zero)
+    coarse_sum1 = every_tile(first_coarse, zero, unroll=6)
 
     @pl.when(has_down)
     def _():
@@ -610,8 +716,8 @@
     def _():
         row_up.wait_send()
 
-    fine_sum2 = every_tile(fine_second, zero)
-    coarse_sum2 = every_tile(second_coarse, zero)
+    fine_sum2 = every_tile(second_fine, zero, unroll=3)
+    coarse_sum2 = every_tile(second_coarse, zero, unroll=6)
     coarse_sum3 = lax.fori_loop(0, tiles, third_coarse, zero, unroll=4)
 
     my_cols = pl.ds(pl.multiple_of(j * wide, LANES), wide)
@@ -685,9 +791,7 @@
     for step in order:
         mine = mine + part_gy[step]
     total = jnp.sum(mine, axis=1, keepdims=True) * (1.0 / sh.cells)
-    norms = jnp.sqrt(total)
-    for s in range(SWEEPS):
-        norm_out[s] = norms[s, 0]
+    norm_out[...] = jnp.broadcast_to(jnp.sqrt(total), (SUB, LANES))
 
     @pl.when(has_right)
     def _():
@@ -699,21 +803,44 @@
 
     @pl.when(has_down)
     def _():
-        for kind in range(3):
+        for kind in range(2):
             fwd_copies[kind][0].wait_send()
+        strip_copies[0].wait_send()
 
     @pl.when(has_up)
     def _():
-        for kind in range(3):
+        for kind in range(2):
             fwd_copies[kind][1].wait_send()
+        strip_copies[1].wait_send()
 
     for step in order:
         for copy in sends[step]:
             copy.wait_send()
+
+    @pl.when((j == 0) | (j == gy - 1))
+    def _():
+        for step in order:
+            strip_of(step, 0).wait_send()
+
     for copy in finals:
         copy.wait()
     for copy in norm_y + norm_x:
         copy.wait_send()
+
+
+def store_kernel(fine, coarse, norms, fine_out, coarse_out, norm_out, scalars, sem):
+    stores = [
+        pltpu.make_async_copy(fine, fine_out, sem.at[0]),
+        pltpu.make_async_copy(coarse, coarse_out, sem.at[1]),
+        pltpu.make_async_copy(scalars, norm_out, sem.at[2]),
+    ]
+    stores[0].start()
+    stores[1].start()
+    for s in range(SWEEPS):
+        scalars[s] = norms[s, 0]
+    stores[2].start()
+    for copy in stores:
+        copy.wait()
 
 
 def solution(mesh):
@@ -732,15 +859,15 @@
             return pltpu.VMEM((*lead, sh.coarse_buf, LANES), F32)
 
         few = sh.halves + 1
-        return pl.pallas_call(
+        fine_v, coarse_v, norm_v = pl.pallas_call(
             functools.partial(kernel, sh),
             out_shape=(
                 pltpu.VMEM(fine_start.shape, F32),
                 pltpu.VMEM(coarse_start.shape, F32),
-                jax.ShapeDtypeStruct((SWEEPS,), F32),
+                pltpu.VMEM((SUB, LANES), F32),
             ),
             in_specs=[in_hbm] * 6,
-            out_specs=(on_chip, on_chip, pl.BlockSpec(memory_space=pltpu.SMEM)),
+            out_specs=(on_chip, on_chip, on_chip),
             scratch_shapes=[
                 pltpu.VMEM((PLANES, sh.slabs, sh.fine_rows, LANES), F32),
                 pltpu.VMEM((PLANES, sh.blocks, sh.slabs * LANES, LANES), F32),
@@ -759,12 +886,17 @@
                 coarse(few),
                 coarse(few),
                 coarse(3, few),
+                coarse(3, few),
+                fine(3),
                 pltpu.VMEM((PLANES, SUB, gy * sh.wide), F32),
                 pltpu.VMEM((PLANES, gy * SUB, LANES), F32),
                 pltpu.VMEM((gy, SUB, LANES), F32),
                 pltpu.VMEM((gy + 2, 3, SUB, sh.wide), F32),
                 pltpu.VMEM((gy + 2, SUB, LANES), F32),
                 pltpu.VMEM((gy + 2, 4, SUB, sh.wide), F32),
+                pltpu.VMEM((gy, SUB, sh.wide), F32),
+                pltpu.VMEM((2, SUB, sh.wide), F32),
+                pltpu.VMEM((2, SUB, sh.wide), F32),
                 pltpu.VMEM((2, PLANES, SUB, LANES), F32),
                 pltpu.VMEM((2, PLANES, SUB, LANES), F32),
                 pltpu.VMEM((gy, 3, SUB, sh.wide), F32),
@@ -781,6 +913,8 @@
                 dma((2, 3)),
                 dma((2, 3)),
                 dma((gy,)),
+                dma((2,)),
+                dma((gy,)),
                 dma((gy,)),
                 dma((2, max(gx, gy))),
                 dma((gy,)),
@@ -791,6 +925,20 @@
             ),
             name="interface_sweeps",
         )(fine_start, fine_known, fine_mu, coarse_start, coarse_known, coarse_mu)
+        anywhere = pl.BlockSpec(memory_space=pl.ANY)
+        return pl.pallas_call(
+            store_kernel,
+            out_shape=(
+                jax.ShapeDtypeStruct(fine_start.shape, F32),
+                jax.ShapeDtypeStruct(coarse_start.shape, F32),
+                jax.ShapeDtypeStruct((SWEEPS,), F32),
+            ),
+            in_specs=[anywhere, anywhere, on_chip],
+            out_specs=(in_hbm, in_hbm, in_hbm),
+            scratch_shapes=[pltpu.SMEM((SWEEPS,), F32), dma((3,))],
+            compiler_params=pltpu.CompilerParams(vmem_limit_bytes=1_000_000),
+            name="store_results",
+        )(fine_v, coarse_v, norm_v)
 
     return jax.shard_map(
         on_device,

time: 46.5 us -> 42.6 us (0.916)
  local copies, waits for them, and re-layouts: 2.41 us -> 0 us
  Pallas kernels: 43.3 us -> 41.8 us
    pallas_call x1, Pallas kernels: 43.3 us -> 40.5 us  [on_device(): pl.pallas_call(functools.partial(kernel, sh), out_shape=(pltpu.VMEM(fine_...]
    unnamed x5 -> x0, local copies, waits for them, and re-layouts: 2.41 us -> none
    pallas_call x0 -> x1, Pallas kernels: none -> 1.3 us  [on_device(): pl.pallas_call(store_kernel, out_shape=(jax.ShapeDtypeStruct(fine_start.s...]
where the time goes in v2:
time: 42.6 us; the launch traced here: 42.5 us
  Pallas kernels  41.8 us (98%)
  between operations  0.64 us (2%)
    pallas_call x1, Pallas kernels, on_device(): pl.pallas_call(functools.partial(kernel, sh), out_shape=(pltpu.VMEM(fine_...  40.5 us
    pallas_call x1, Pallas kernels, on_device(): pl.pallas_call(store_kernel, out_shape=(jax.ShapeDtypeStruct(fine_start.s...  1.3 us

profile of v2, /device:TPU:1, one launch (start us, length us, event | category | flops | bytes accessed | tf_op | source)
XLA Modules:
  0.0 42.5 jit_solution(10378425856522834852)
XLA Ops:
  0.6 40.5 %interface_sweeps.1 = (f32[3,256,512]{2,1,0:T(8,128)S(1)}, f32[3,8,4096]{2,1,0:T(8,128)S(1)}, f32[8,128]{1,0:T(8,128)S(1)}) custom-call(f32[3,256,512]{2,1,0:T(8,128)} %fine_start.1, f32[3,256,512]{2,1,0:T(8,128)} %fine_known.1, f32[256,512]{1,0:T(8,128)} %fine_mu.1, f32[3,8,4096]{2,1,0:T(8,128)} %coarse_start.1, f32[3,8,4096]{2,1,0:T(8,128)} %coarse_known.1, ...), custom_call_target="tpu_custom_call" | custom-call | tf_op jit(solution)/shard_map/interface_sweeps/pallas_call | solution.py:862
  41.2 1.3 %store_results.1 = (f32[3,256,512]{2,1,0:T(8,128)}, f32[3,8,4096]{2,1,0:T(8,128)}, f32[3]{0:T(128)}) custom-call(f32[3,256,512]{2,1,0:T(8,128)S(1)} %get-tuple-element.6.fine, f32[3,8,4096]{2,1,0:T(8,128)S(1)} %get-tuple-element.7.coarse, f32[8,128]{1,0:T(8,128)S(1)} %get-tuple-element.8.norms), custom_call_target="tpu_custom_call" | custom-call | tf_op jit(solution)/shard_map/store_results/pallas_call | solution.py:929

commit v3 on v2

--- a/solution.py
+++ b/solution.py
@@ -33,8 +33,25 @@
         self.cells = 3.0 * gx * gy * fine_rows * fine_cols * 1.25
 
 
+RING = 4
+
+
+def hops(step):
+    return sum(min(d, RING - d) for d in divmod(step, RING))
+
+
 def far_first(count):
-    return sorted(range(1, count), key=lambda step: -min(step, count - step))
+    return sorted(range(1, count), key=lambda step: -hops(step))
+
+
+def torus_add(at, step):
+    row, column = at // RING + step // RING, lax.rem(at, RING) + step % RING
+    return lax.rem(row, RING) * RING + lax.rem(column, RING)
+
+
+def torus_back(at, step):
+    row, column = at // RING + RING - step // RING, lax.rem(at, RING) + RING - step % RING
+    return lax.rem(row, RING) * RING + lax.rem(column, RING)
 
 
 def lane_iota():
@@ -158,9 +175,9 @@
     barrier = pltpu.get_barrier_semaphore()
     for step in far_first(gy):
         pl.semaphore_signal(
-            barrier, inc=1, device_id=(i, lax.rem(j + step, gy)), device_id_type=MESH
+            barrier, inc=1, device_id=(i, torus_add(j, step)), device_id_type=MESH
         )
-    for step in far_first(gx):
+    for step in range(1, gx):
         pl.semaphore_signal(
             barrier, inc=1, device_id=(lax.rem(i + step, gx), j), device_id_type=MESH
         )
@@ -267,7 +284,7 @@
         edge_left.start()
 
     def sends_of(step):
-        to = lax.rem(j + step, gy)
+        to = torus_add(j, step)
         cols = pl.ds(pl.multiple_of(to * wide, LANES), wide)
         ends = (
             (own.at[pl.ds(0, 3), :, cols], got_c),
@@ -279,10 +296,10 @@
             for n, (src, dst) in enumerate(ends)
         ]
 
-    order = list(range(1, gy))
+    order = far_first(gy)
     sends = {step: sends_of(step) for step in order}
     def strip_of(step, side):
-        to = lax.rem(j + step, gy)
+        to = torus_add(j, step)
         return remote(
             strip_out.at[to], strip_in.at[side], strip_send.at[step], strip_recv.at[side], i, to
         )
@@ -311,7 +328,11 @@
             else:
                 got_k[j + 1, p - 3, :, pl.ds(LANES * u, LANES)] = piece
 
+    def scale_of(p):
+        return jnp.where((p >= 3) & (p < 6), 4.0, 1.0).astype(F32)
+
     def split_columns(p, carry):
+        scale = scale_of(p)
         for b in range(sh.blocks):
             rows = pl.ds(LANES * b, LANES)
             for t in range(1, slabs - 1):
@@ -320,7 +341,7 @@
             rows = pl.ds(FINE_OFF + LANES * b, LANES)
             for s in range(slabs):
                 begin = 2 * LANES * (s // 2) + s % 2
-                f_a[p, s, rows, :] = turned[p, b, pl.ds(begin, LANES, stride=2), :].T
+                f_a[p, s, rows, :] = turned[p, b, pl.ds(begin, LANES, stride=2), :].T * scale
         return carry
 
     lax.fori_loop(0, PLANES, split_columns, 0)
@@ -339,7 +360,7 @@
         for b in range(sh.blocks):
             from_left = edge_in[0, p, pl.ds(EDGE * b, EDGE), :]
             from_right = edge_in[1, p, pl.ds(EDGE * b, EDGE), :]
-            slab = jnp.concatenate([from_right, between, from_left], axis=0).T
+            slab = jnp.concatenate([from_right, between, from_left], axis=0).T * scale_of(p)
             f_a[p, halo, pl.ds(FINE_OFF + LANES * b, LANES), :] = slab
         return carry
 
@@ -380,12 +401,14 @@
     def swapped_pairs(value):
         return jnp.where(even, pltpu.roll(value, LANES - 1, 1), pltpu.roll(value, 1, 1))
 
-    def produce(k, row, values, c_ref, q_ref, w_ref):
+    def produce(k, row, values, c_ref, q_ref, w_ref, inner=False):
         right = [pltpu.roll(v, 1, 1) for v in values]
         left = [pltpu.roll(v, LANES - 1, 1) for v in values]
         rows = pl.ds(row, SUB)
         count = len(values)
         for t, value in enumerate(values):
+            if t == coarse_halo and inner:
+                continue
             before = jnp.where(first, right[t - 1], right[t])
             after = jnp.where(last, left[(t + 1) % count], left[t])
             c_ref[k, t, rows, :] = value
@@ -413,15 +436,15 @@
         rows = pl.ds(coarse_row(slot - 1), SUB)
         held = ((slot > 0) | has_up) & ((slot <= gy) | has_down)
         for k in range(3):
-            ckh[k, rows, :] = halo_of(slot, 3 + k)
+            ckh[k, rows, :] = 4.0 * halo_of(slot, 3 + k)
         for t in range(halves + 1):
             if t == coarse_halo:
                 value, valid = halo_of(slot, 6), halo_lanes & held
             else:
                 value, valid = got_k[slot, 3, :, pl.ds(LANES * t, LANES)], (lane >= 0) & held
             diag = value + 1.0
-            cd[t, rows, :] = diag
-            ci[t, rows, :] = jnp.where(valid, 1.0 / diag, 0.0)
+            cd[t, rows, :] = diag * diag
+            ci[t, rows, :] = jnp.where(valid, 0.25 * (1.0 / diag), 0.0)
         return carry
 
     fwd_copies = {}
@@ -455,8 +478,15 @@
             for p in range(4):
                 got_k[gy + 1, p, pl.ds(0, 2), :] = strip_far[1, pl.ds(2 * p, 2), :]
 
-    def wait_from(kinds, source):
-        step = lax.rem(j - source + gy, gy)
+    def wait_step(kinds, step):
+        source = torus_back(j, step)
+        for kind in kinds:
+            dst = (got_c, got_p, got_k)[kind].at[source + 1]
+            remote(dst, dst, a_send.at[kind, step], a_recv.at[kind, step], i, source).wait_recv()
+
+    def wait_source(kinds, source):
+        step = RING * lax.rem(j // RING + RING - source // RING, RING)
+        step = step + lax.rem(lax.rem(j, RING) + RING - source % RING, RING)
 
         @pl.when(step > 0)
         def _():
@@ -464,46 +494,33 @@
                 dst = (got_c, got_p, got_k)[kind].at[source + 1]
                 remote(dst, dst, a_send.at[kind, step], a_recv.at[kind, step], i, source).wait_recv()
 
-    def pass_on(kinds):
-        wait_from(kinds, gy - 1)
+    def pass_on(source):
+        wait_source((0, 1), source)
+        side, there = (0, has_down) if source else (1, has_up)
+
+        @pl.when(there)
+        def _():
+            fwd_copies[0][side].start()
+            fwd_copies[1][side].start()
+
+    def passed_on():
+        @pl.when(has_up)
+        def _():
+            fwd_copies[0][0].wait_recv()
+            fwd_copies[1][0].wait_recv()
 
         @pl.when(has_down)
         def _():
-            for kind in kinds:
-                fwd_copies[kind][0].start()
-
-        wait_from(kinds, 0)
-
-        @pl.when(has_up)
-        def _():
-            for kind in kinds:
-                fwd_copies[kind][1].start()
-
-    def wait_rest(kinds):
-        def rest(source, carry):
-            wait_from(kinds, source)
-            return carry
-
-        lax.fori_loop(1, gy - 1, rest, 0)
-
-    def passed_on(kinds):
-        @pl.when(has_up)
-        def _():
-            for kind in kinds:
-                fwd_copies[kind][0].wait_recv()
-
-        @pl.when(has_down)
-        def _():
-            for kind in kinds:
-                fwd_copies[kind][1].wait_recv()
+            fwd_copies[0][1].wait_recv()
+            fwd_copies[1][1].wait_recv()
 
     def diagonal(row, held):
         rows = pl.ds(row, SUB)
         for t in range(slabs + 1):
             diag = f_a[6, t, rows, :] + 1.0
             valid = (halo_lanes_fine if t == halo else (lane >= 0)) & held
-            fd[t, rows, :] = diag
-            fi[t, rows, :] = jnp.where(valid, 1.0 / diag, 0.0)
+            fd[t, rows, :] = diag * diag
+            fi[t, rows, :] = jnp.where(valid, 0.25 * (1.0 / diag), 0.0)
 
     def diagonals(step, carry):
         for n in range(4):
@@ -512,29 +529,20 @@
 
     lax.fori_loop(0, sh.fine_rows // (4 * SUB), diagonals, 0)
 
-    pass_on((0, 1))
-    wait_rest((0, 1))
-    lax.fori_loop(1, gy + 1, spread_first, 0, unroll=4)
-
-    pass_strips_on()
-    @pl.when(has_up)
-    def _():
-        row_down.wait_recv()
-
-    @pl.when(has_down)
-    def _():
-        row_up.wait_recv()
-
-    for row, held in (
-        (FINE_OFF - 16, lane < 0),
-        (FINE_OFF - 8, (lane >= 0) & has_up),
-        (fine_end, (lane >= 0) & has_down),
-        (fine_end + 8, lane < 0),
-    ):
-        diagonal(row, held)
-
-    passed_on((0, 1))
-    lax.fori_loop(0, 2, lambda e, c: spread_first((gy + 1) * e, c), 0, unroll=2)
+    pass_on(gy - 1)
+    pass_on(0)
+    group = 4
+    for begin in range(0, gy, group):
+        if begin == gy // 2:
+            pass_strips_on()
+        sources = []
+        for step in ([0] + order)[begin : begin + group]:
+            source = torus_back(j, step) if step else j
+            if step:
+                pl.when((source > 0) & (source < gy - 1))(lambda: wait_step((0, 1), step))
+            sources.append(source)
+        for source in sources:
+            spread_first(source + 1, 0)
 
     def beside(values):
         side = values[halo]
@@ -552,12 +560,24 @@
         )
         return sums
 
+    def squares(parts, scales, acc):
+        for part_sum, scale in zip(parts, scales):
+            acc = acc + part_sum * scale
+        return acc
+
+    def grown(total, new, old):
+        step = new - old
+        return step * step if total is None else total + step * step
+
     def fine_tile(m, acc, f_in, q_ref, f_out, count):
         base = FINE_OFF + 16 * m
         upper, lower = pl.ds(base, SUB, stride=2), pl.ds(base + 1, SUB, stride=2)
         above, below = pl.ds(base - 1, SUB, stride=2), pl.ds(base + 2, SUB, stride=2)
         crow = COARSE_OFF + SUB * m
         q_here, q_up, q_down = pl.ds(crow, SUB), pl.ds(crow - 1, SUB), pl.ds(crow + 1, SUB)
+        inv_top = [fi[t, upper, :] for t in range(count)]
+        inv_low = [fi[t, lower, :] for t in range(count)]
+        part_top, part_low = [None] * slabs, [None] * slabs
         for k in range(3):
             tops = [f_in[k, t, upper, :] for t in range(slabs + 1)]
             lows = [f_in[k, t, lower, :] for t in range(slabs + 1)]
@@ -565,16 +585,16 @@
             for t in range(count):
                 three = 3.0 * q_ref[k, t, q_here, :]
                 nb = (lows[t] + f_in[k, t, above, :]) + (top_sum[t] + q_ref[k, t, q_up, :])
-                total = f_a[3 + k, t, upper, :] + 0.25 * (nb + three)
-                res = total - fd[t, upper, :] * tops[t]
-                f_out[k, t, upper, :] = total * fi[t, upper, :]
+                new = (f_a[3 + k, t, upper, :] + (nb + three)) * inv_top[t]
+                f_out[k, t, upper, :] = new
                 nb2 = (tops[t] + f_in[k, t, below, :]) + (low_sum[t] + q_ref[k, t, q_down, :])
-                total2 = f_a[3 + k, t, lower, :] + 0.25 * (nb2 + three)
-                res2 = total2 - fd[t, lower, :] * lows[t]
-                f_out[k, t, lower, :] = total2 * fi[t, lower, :]
-                if acc is not None and t < slabs:
-                    acc = acc + (res * res + res2 * res2)
-        return acc
+                new2 = (f_a[3 + k, t, lower, :] + (nb2 + three)) * inv_low[t]
+                f_out[k, t, lower, :] = new2
+                if t < slabs:
+                    part_top[t] = grown(part_top[t], new, tops[t])
+                    part_low[t] = grown(part_low[t], new2, lows[t])
+        acc = squares(part_top, [fd[t, upper, :] for t in range(slabs)], acc)
+        return squares(part_low, [fd[t, lower, :] for t in range(slabs)], acc)
 
     def coarse_sum(m, k, t, f_in, c_ref, w_ref):
         base = FINE_OFF + 16 * m
@@ -586,19 +606,29 @@
             four = (f_in[k, 2 * t, upper, :] + f_in[k, 2 * t, lower, :]) + (
                 f_in[k, 2 * t + 1, upper, :] + f_in[k, 2 * t + 1, lower, :]
             )
-        return 0.25 * (coarse_near(m, k, t, c_ref, w_ref) + 0.5 * four)
-
-    def coarse_step(m, k, t, acc, added, c_ref):
+        return coarse_near(m, k, t, c_ref, w_ref) + 0.5 * four
+
+    def coarse_step(m, k, t, added, inv):
         rows = pl.ds(coarse_row(m), SUB)
         if t == coarse_halo:
             known = ckh[k, rows, :]
         else:
-            known = got_k[m + 1, k, :, pl.ds(LANES * t, LANES)]
-        total = known + added
-        if acc is not None and t < halves:
-            res = total - cd[t, rows, :] * c_ref[k, t, rows, :]
-            acc = acc + res * res
-        return total * ci[t, rows, :], acc
+            known = 4.0 * got_k[m + 1, k, :, pl.ds(LANES * t, LANES)]
+        return (known + added) * inv
+
+    def coarse_tile(m, acc, added_of, c_ref, count, use):
+        rows = pl.ds(coarse_row(m), SUB)
+        inv = [ci[t, rows, :] for t in range(count)]
+        parts = [None] * halves
+        for k in range(3):
+            values = []
+            for t in range(count):
+                value = coarse_step(m, k, t, added_of(k, t), inv[t])
+                values.append(value)
+                if t < halves:
+                    parts[t] = grown(parts[t], value, c_ref[k, t, rows, :])
+            use(k, values)
+        return squares(parts, [cd[t, rows, :] for t in range(halves)], acc)
 
     def near_sum(m, carry):
         base = FINE_OFF + 16 * m
@@ -611,14 +641,14 @@
             both = [tops[t] + lows[t] for t in range(slabs + 1)]
             for t in range(slabs + 1):
                 nb = (lows[t] + f_b[k, t, above, :]) + top_sum[t]
-                near[k, t, upper, :] = f_a[3 + k, t, upper, :] + 0.25 * nb
+                near[k, t, upper, :] = f_a[3 + k, t, upper, :] + nb
                 nb2 = (tops[t] + f_b[k, t, below, :]) + low_sum[t]
-                near[k, t, lower, :] = f_a[3 + k, t, lower, :] + 0.25 * nb2
+                near[k, t, lower, :] = f_a[3 + k, t, lower, :] + nb2
             rows = pl.ds(coarse_row(m), SUB)
             for t in range(halves):
-                pre_b[k, t, rows, :] = 0.125 * (both[2 * t] + both[2 * t + 1])
+                pre_b[k, t, rows, :] = 0.5 * (both[2 * t] + both[2 * t + 1])
             side = both[halo]
-            pre_b[k, coarse_halo, rows, :] = 0.125 * (side + swapped_pairs(side))
+            pre_b[k, coarse_halo, rows, :] = 0.5 * (side + swapped_pairs(side))
         return zero
 
     def second_fine(m, acc):
@@ -626,17 +656,20 @@
         upper, lower = pl.ds(base, SUB, stride=2), pl.ds(base + 1, SUB, stride=2)
         crow = COARSE_OFF + SUB * m
         q_here, q_up, q_down = pl.ds(crow, SUB), pl.ds(crow - 1, SUB), pl.ds(crow + 1, SUB)
-        for k in range(3):
-            for t in range(slabs + 1):
-                three = 0.75 * q_b[k, t, q_here, :]
-                total = near[k, t, upper, :] + (three + 0.25 * q_b[k, t, q_up, :])
-                res = total - fd[t, upper, :] * f_b[k, t, upper, :]
-                f_a[k, t, upper, :] = total * fi[t, upper, :]
-                total2 = near[k, t, lower, :] + (three + 0.25 * q_b[k, t, q_down, :])
-                res2 = total2 - fd[t, lower, :] * f_b[k, t, lower, :]
-                f_a[k, t, lower, :] = total2 * fi[t, lower, :]
+        for t in range(slabs + 1):
+            inv_top, inv_low = fi[t, upper, :], fi[t, lower, :]
+            part_top, part_low = None, None
+            for k in range(3):
+                three = 3.0 * q_b[k, t, q_here, :]
+                new = (near[k, t, upper, :] + (three + q_b[k, t, q_up, :])) * inv_top
+                f_a[k, t, upper, :] = new
+                new2 = (near[k, t, lower, :] + (three + q_b[k, t, q_down, :])) * inv_low
+                f_a[k, t, lower, :] = new2
                 if t < slabs:
-                    acc = acc + (res * res + res2 * res2)
+                    part_top = grown(part_top, new, f_b[k, t, upper, :])
+                    part_low = grown(part_low, new2, f_b[k, t, lower, :])
+            if t < slabs:
+                acc = acc + (part_top * fd[t, upper, :] + part_low * fd[t, lower, :])
         return acc
 
     def coarse_near(m, k, t, c_ref, w_ref):
@@ -653,32 +686,32 @@
 
     def first_coarse(m, acc):
         rows = pl.ds(coarse_row(m), SUB)
-        for k in range(3):
-            values = []
-            for t in range(halves + 1):
-                value, acc = coarse_step(m, k, t, acc, pre[k, t, rows, :], c_a)
-                values.append(value)
+
+        def use(k, values):
             produce(k, coarse_row(m), values, c_b, q_b, w_b)
-        return acc
+
+        return coarse_tile(m, acc, lambda k, t: pre[k, t, rows, :], c_a, halves + 1, use)
 
     def second_coarse(m, acc):
-        for k in range(3):
-            values = []
-            for t in range(halves + 1):
-                added = pre_b[k, t, pl.ds(coarse_row(m), SUB), :]
-                added = added + 0.25 * coarse_near(m, k, t, c_b, w_b)
-                value, acc = coarse_step(m, k, t, acc, added, c_b)
-                values.append(value)
-            produce(k, coarse_row(m), values, c_a, q_a, w_a)
-        return acc
+        rows = pl.ds(coarse_row(m), SUB)
+
+        def added_of(k, t):
+            return pre_b[k, t, rows, :] + coarse_near(m, k, t, c_b, w_b)
+
+        def use(k, values):
+            produce(k, coarse_row(m), values, c_a, q_a, w_a, inner=True)
+
+        return coarse_tile(m, acc, added_of, c_b, halves + 1, use)
 
     def third_coarse(m, acc):
-        for k in range(3):
-            for t in range(halves):
-                added = coarse_sum(m, k, t, f_a, c_a, w_a)
-                value, acc = coarse_step(m, k, t, acc, added, c_a)
+        def added_of(k, t):
+            return coarse_sum(m, k, t, f_a, c_a, w_a)
+
+        def use(k, values):
+            for t, value in enumerate(values):
                 fin[m, k, :, pl.ds(LANES * t, LANES)] = value
-        return acc
+
+        return coarse_tile(m, acc, added_of, c_a, halves, use)
 
     def every_tile(body, acc, unroll=6):
         def step(n, acc):
@@ -695,13 +728,47 @@
     def fine_third(m, acc):
         return fine_tile(m, acc, f_a, q_a, f_b, slabs)
 
-    fine_sum1 = every_tile(fine_first, zero)
-    every_tile(first_sum, zero)
+    def both_first(m, acc):
+        first_sum(m, 0)
+        return fine_first(m, acc)
+
+    fine_sum1 = lax.fori_loop(1, tiles - 1, fine_first, zero, unroll=7)
+    lax.fori_loop(1, tiles - 1, first_sum, zero, unroll=7)
+
+    @pl.when(has_up)
+    def _():
+        row_down.wait_recv()
+
+    @pl.when(has_down)
+    def _():
+        row_up.wait_recv()
+
+    for row, held in (
+        (FINE_OFF - 16, lane < 0),
+        (FINE_OFF - 8, (lane >= 0) & has_up),
+        (fine_end, (lane >= 0) & has_down),
+        (fine_end + 8, lane < 0),
+    ):
+        diagonal(row, held)
+
+    passed_on()
+    lax.fori_loop(0, 2, lambda e, c: spread_first((gy + 1) * e, c), 0, unroll=2)
+
+    def outer_first(e, acc):
+        for n in range(2):
+            m = jnp.where(e == 0, n - 1, tiles - 1 + n)
+            part_sum = both_first(m, zero)
+            if n == 0:
+                acc = acc + jnp.where(e == 1, 1.0, 0.0).astype(F32) * part_sum
+            else:
+                acc = acc + jnp.where(e == 0, 1.0, 0.0).astype(F32) * part_sum
+        return acc
+
+    fine_sum1 = lax.fori_loop(0, 2, outer_first, fine_sum1, unroll=2)
     every_tile(near_sum, zero)
 
-    wait_from((2,), 0)
-    wait_from((2,), gy - 1)
-    wait_rest((2,))
+    for step in order:
+        wait_step((2,), step)
     lax.fori_loop(1, gy + 1, spread_second, 0, unroll=8)
     strips_passed_on()
     lax.fori_loop(0, 2, lambda e, c: spread_second((gy + 1) * e, c), 0, unroll=2)
@@ -723,7 +790,7 @@
     my_cols = pl.ds(pl.multiple_of(j * wide, LANES), wide)
     finals = []
     for step in order:
-        to = lax.rem(j + step, gy)
+        to = torus_add(j, step)
         copy = remote(
             fin.at[to], coarse_out.at[:, :, my_cols], fin_send.at[step], fin_recv.at[step], i, to
         )
@@ -782,7 +849,7 @@
             norm_send.at[1, step],
             norm_recv_y.at[step],
             i,
-            lax.rem(j + step, gy),
+            torus_add(j, step),
         )
         copy.start()
         norm_y.append(copy)

time: 42.6 us -> 40.4 us (0.948)
  Pallas kernels: 41.8 us -> 39.7 us
    pallas_call x1, Pallas kernels: 40.5 us -> 38.4 us  [on_device(): pl.pallas_call(functools.partial(kernel, sh), out_shape=(pltpu.VMEM(fine_...]
where the time goes in v3:
time: 40.4 us; the launch traced here: 40.3 us
  Pallas kernels  39.7 us (98%)
  between operations  0.64 us (2%)
    pallas_call x1, Pallas kernels, on_device(): pl.pallas_call(functools.partial(kernel, sh), out_shape=(pltpu.VMEM(fine_...  38.4 us
    pallas_call x1, Pallas kernels, on_device(): pl.pallas_call(store_kernel, out_shape=(jax.ShapeDtypeStruct(fine_start.s...  1.3 us

profile of v3, /device:TPU:1, one launch (start us, length us, event | category | flops | bytes accessed | tf_op | source)
XLA Modules:
  0.0 40.3 jit_solution(6954666187172609310)
XLA Ops:
  0.6 38.4 %interface_sweeps.1 = (f32[3,256,512]{2,1,0:T(8,128)S(1)}, f32[3,8,4096]{2,1,0:T(8,128)S(1)}, f32[8,128]{1,0:T(8,128)S(1)}) custom-call(f32[3,256,512]{2,1,0:T(8,128)} %fine_start.1, f32[3,256,512]{2,1,0:T(8,128)} %fine_known.1, f32[256,512]{1,0:T(8,128)} %fine_mu.1, f32[3,8,4096]{2,1,0:T(8,128)} %coarse_start.1, f32[3,8,4096]{2,1,0:T(8,128)} %coarse_known.1, ...), custom_call_target="tpu_custom_call" | custom-call | tf_op jit(solution)/shard_map/interface_sweeps/pallas_call | solution.py:929
  39.0 1.3 %store_results.1 = (f32[3,256,512]{2,1,0:T(8,128)}, f32[3,8,4096]{2,1,0:T(8,128)}, f32[3]{0:T(128)}) custom-call(f32[3,256,512]{2,1,0:T(8,128)S(1)} %get-tuple-element.6.fine, f32[3,8,4096]{2,1,0:T(8,128)S(1)} %get-tuple-element.7.coarse, f32[8,128]{1,0:T(8,128)S(1)} %get-tuple-element.8.norms), custom_call_target="tpu_custom_call" | custom-call | tf_op jit(solution)/shard_map/store_results/pallas_call | solution.py:996

commit v4 on v3

--- a/solution.py
+++ b/solution.py
@@ -315,8 +315,6 @@
 
     pl.when(j == gy - 1)(lambda: send_strips(0))
     pl.when(j == 0)(lambda: send_strips(1))
-    for step in order:
-        sends[step][2].start()
 
     got_p[j + 1] = pack[j]
     for u in range(halves):
@@ -484,24 +482,16 @@
             dst = (got_c, got_p, got_k)[kind].at[source + 1]
             remote(dst, dst, a_send.at[kind, step], a_recv.at[kind, step], i, source).wait_recv()
 
-    def wait_source(kinds, source):
-        step = RING * lax.rem(j // RING + RING - source // RING, RING)
-        step = step + lax.rem(lax.rem(j, RING) + RING - source % RING, RING)
-
-        @pl.when(step > 0)
+    def pass_on(source):
+        @pl.when((source == gy - 1) & has_down)
         def _():
-            for kind in kinds:
-                dst = (got_c, got_p, got_k)[kind].at[source + 1]
-                remote(dst, dst, a_send.at[kind, step], a_recv.at[kind, step], i, source).wait_recv()
-
-    def pass_on(source):
-        wait_source((0, 1), source)
-        side, there = (0, has_down) if source else (1, has_up)
-
-        @pl.when(there)
+            fwd_copies[0][0].start()
+            fwd_copies[1][0].start()
+
+        @pl.when((source == 0) & has_up)
         def _():
-            fwd_copies[0][side].start()
-            fwd_copies[1][side].start()
+            fwd_copies[0][1].start()
+            fwd_copies[1][1].start()
 
     def passed_on():
         @pl.when(has_up)
@@ -529,20 +519,21 @@
 
     lax.fori_loop(0, sh.fine_rows // (4 * SUB), diagonals, 0)
 
-    pass_on(gy - 1)
-    pass_on(0)
     group = 4
     for begin in range(0, gy, group):
         if begin == gy // 2:
-            pass_strips_on()
+            for step in order:
+                sends[step][2].start()
         sources = []
         for step in ([0] + order)[begin : begin + group]:
             source = torus_back(j, step) if step else j
             if step:
-                pl.when((source > 0) & (source < gy - 1))(lambda: wait_step((0, 1), step))
+                wait_step((0, 1), step)
+            pass_on(source)
             sources.append(source)
         for source in sources:
             spread_first(source + 1, 0)
+    pass_strips_on()
 
     def beside(values):
         side = values[halo]
@@ -773,8 +764,6 @@
     strips_passed_on()
     lax.fori_loop(0, 2, lambda e, c: spread_second((gy + 1) * e, c), 0, unroll=2)
 
-    coarse_sum1 = every_tile(first_coarse, zero, unroll=6)
-
     @pl.when(has_down)
     def _():
         row_down.wait_send()
@@ -783,8 +772,26 @@
     def _():
         row_up.wait_send()
 
-    fine_sum2 = every_tile(second_fine, zero, unroll=3)
-    coarse_sum2 = every_tile(second_coarse, zero, unroll=6)
+    def inner_share(m):
+        return jnp.where((m >= 0) & (m < tiles), 1.0, 0.0).astype(F32)
+
+    def lead(m, sums):
+        share = inner_share(m)
+        return (sums[0] + share * first_coarse(m, zero), sums[1], sums[2])
+
+    def follow(m, sums):
+        share = inner_share(m)
+        fine_part = second_fine(m, zero)
+        coarse_part = second_coarse(m, zero)
+        return (sums[0], sums[1] + share * fine_part, sums[2] + share * coarse_part)
+
+    def lead_and_follow(m, sums):
+        return lead(m + 1, follow(m - 1, sums))
+
+    sums = lax.fori_loop(-1, 1, lead, (zero, zero, zero), unroll=2)
+    sums = lax.fori_loop(0, tiles, lead_and_follow, sums, unroll=4)
+    sums = lax.fori_loop(tiles - 1, tiles + 1, follow, sums, unroll=2)
+    coarse_sum1, fine_sum2, coarse_sum2 = sums
     coarse_sum3 = lax.fori_loop(0, tiles, third_coarse, zero, unroll=4)
 
     my_cols = pl.ds(pl.multiple_of(j * wide, LANES), wide)

time: 40.4 us -> 40.1 us (level)
  no operation moved by 1% of the time
where the time goes in v4:
time: 40.1 us; the launch traced here: 40 us
  Pallas kernels  39.4 us (98%)
  between operations  0.64 us (2%)
    pallas_call x1, Pallas kernels, on_device(): pl.pallas_call(functools.partial(kernel, sh), out_shape=(pltpu.VMEM(fine_...  38.1 us
    pallas_call x1, Pallas kernels, on_device(): pl.pallas_call(store_kernel, out_shape=(jax.ShapeDtypeStruct(fine_start.s...  1.3 us

profile of v4, /device:TPU:1, one launch (start us, length us, event | category | flops | bytes accessed | tf_op | source)
XLA Modules:
  0.0 40.0 jit_solution(12703919976426565691)
XLA Ops:
  0.6 38.1 %interface_sweeps.1 = (f32[3,256,512]{2,1,0:T(8,128)S(1)}, f32[3,8,4096]{2,1,0:T(8,128)S(1)}, f32[8,128]{1,0:T(8,128)S(1)}) custom-call(f32[3,256,512]{2,1,0:T(8,128)} %fine_start.1, f32[3,256,512]{2,1,0:T(8,128)} %fine_known.1, f32[256,512]{1,0:T(8,128)} %fine_mu.1, f32[3,8,4096]{2,1,0:T(8,128)} %coarse_start.1, f32[3,8,4096]{2,1,0:T(8,128)} %coarse_known.1, ...), custom_call_target="tpu_custom_call" | custom-call | tf_op jit(solution)/shard_map/interface_sweeps/pallas_call | solution.py:936
  38.7 1.3 %store_results.1 = (f32[3,256,512]{2,1,0:T(8,128)}, f32[3,8,4096]{2,1,0:T(8,128)}, f32[3]{0:T(128)}) custom-call(f32[3,256,512]{2,1,0:T(8,128)S(1)} %get-tuple-element.6.fine, f32[3,8,4096]{2,1,0:T(8,128)S(1)} %get-tuple-element.7.coarse, f32[8,128]{1,0:T(8,128)S(1)} %get-tuple-element.8.norms), custom_call_target="tpu_custom_call" | custom-call | tf_op jit(solution)/shard_map/store_results/pallas_call | solution.py:1003

commit v5 on v4

--- a/solution.py
+++ b/solution.py
@@ -124,11 +124,8 @@
     fwd_recv,
     strip_send,
     strip_recv,
-    fin_send,
-    fin_recv,
-    norm_send,
-    norm_recv_y,
-    norm_recv_x,
+    fin_sem,
+    norm_sem,
 ):
     gx, gy = sh.gx, sh.gy
     i = lax.axis_index("gx")
@@ -152,25 +149,17 @@
             device_id_type=MESH,
         )
 
-    loads = []
-
-    def load(src, dst):
-        copy = pltpu.make_async_copy(src, dst, load_sem.at[len(loads)])
-        copy.start()
-        loads.append(copy)
-        return copy
-
-    own_loads = [
-        load(coarse_start, own.at[pl.ds(0, 3)]),
-        load(coarse_known, own.at[pl.ds(3, 3)]),
-        load(coarse_mu, own.at[6]),
-    ]
-    fine_loads = []
+    def load(src, dst, kind):
+        pltpu.make_async_copy(src, dst, load_sem.at[kind]).start()
+
+    load(coarse_start, own.at[pl.ds(0, 3)], 0)
+    load(coarse_known, own.at[pl.ds(3, 3)], 0)
+    load(coarse_mu, own.at[6], 0)
     for t in [0, slabs - 1] + list(range(1, slabs - 1)):
         cols = pl.ds(LANES * t, LANES)
-        fine_loads.append(load(fine_start.at[:, :, cols], nat.at[pl.ds(0, 3), t]))
-        fine_loads.append(load(fine_known.at[:, :, cols], nat.at[pl.ds(3, 3), t]))
-        fine_loads.append(load(fine_mu.at[:, cols], nat.at[6, t]))
+        load(fine_start.at[:, :, cols], nat.at[pl.ds(0, 3), t], 1)
+        load(fine_known.at[:, :, cols], nat.at[pl.ds(3, 3), t], 1)
+        load(fine_mu.at[:, cols], nat.at[6, t], 1)
 
     barrier = pltpu.get_barrier_semaphore()
     for step in far_first(gy):
@@ -221,8 +210,7 @@
     pl.when(j == 0)(lambda: clear_columns(0))
     pl.when(j == gy - 1)(lambda: clear_columns(1))
 
-    for copy in own_loads:
-        copy.wait()
+    pltpu.make_async_copy(own, own, load_sem.at[0]).wait()
 
     for dest in range(gy):
         for p in range(PLANES):
@@ -250,8 +238,7 @@
     pl.when(j == gy - 1)(lambda: pack_strip(SUB - 2))
     pl.when(j == 0)(lambda: pack_strip(0))
 
-    for copy in fine_loads:
-        copy.wait()
+    pltpu.make_async_copy(nat, nat, load_sem.at[1]).wait()
 
     def turn_edges(p, carry):
         for b in range(sh.blocks):
@@ -292,16 +279,28 @@
             (own.at[pl.ds(3, 4), :, cols], got_k),
         )
         return [
-            remote(src, dst.at[j + 1], a_send.at[n, step], a_recv.at[n, step], i, to)
+            remote(src, dst.at[j + 1], a_send.at[n], a_recv.at[n, group_of(n, step)], i, to)
             for n, (src, dst) in enumerate(ends)
         ]
 
     order = far_first(gy)
+    peers = gy - 1
+    group = 4
+
+    def group_of(kind, step):
+        return 0 if kind == 2 else (1 + order.index(step)) // group
+
+    def all_sent(ref, sem):
+        remote(ref, ref, sem, sem, i, j).wait_send()
+
+    def all_here(ref, sem):
+        remote(ref, ref, sem, sem, i, j).wait_recv()
+
     sends = {step: sends_of(step) for step in order}
     def strip_of(step, side):
         to = torus_add(j, step)
         return remote(
-            strip_out.at[to], strip_in.at[side], strip_send.at[step], strip_recv.at[side], i, to
+            strip_out.at[to], strip_in.at[side], strip_send.at[0], strip_recv.at[side], i, to
         )
 
     for step in order:
@@ -476,12 +475,6 @@
             for p in range(4):
                 got_k[gy + 1, p, pl.ds(0, 2), :] = strip_far[1, pl.ds(2 * p, 2), :]
 
-    def wait_step(kinds, step):
-        source = torus_back(j, step)
-        for kind in kinds:
-            dst = (got_c, got_p, got_k)[kind].at[source + 1]
-            remote(dst, dst, a_send.at[kind, step], a_recv.at[kind, step], i, source).wait_recv()
-
     def pass_on(source):
         @pl.when((source == gy - 1) & has_down)
         def _():
@@ -519,18 +512,17 @@
 
     lax.fori_loop(0, sh.fine_rows // (4 * SUB), diagonals, 0)
 
-    group = 4
     for begin in range(0, gy, group):
         if begin == gy // 2:
             for step in order:
                 sends[step][2].start()
-        sources = []
-        for step in ([0] + order)[begin : begin + group]:
-            source = torus_back(j, step) if step else j
-            if step:
-                wait_step((0, 1), step)
+        steps = ([0] + order)[begin : begin + group]
+        count = len(steps) - steps.count(0)
+        all_here(got_c.at[pl.ds(0, count)], a_recv.at[0, begin // group])
+        all_here(got_p.at[pl.ds(0, count)], a_recv.at[1, begin // group])
+        sources = [torus_back(j, step) if step else j for step in steps]
+        for source in sources:
             pass_on(source)
-            sources.append(source)
         for source in sources:
             spread_first(source + 1, 0)
     pass_strips_on()
@@ -758,8 +750,7 @@
     fine_sum1 = lax.fori_loop(0, 2, outer_first, fine_sum1, unroll=2)
     every_tile(near_sum, zero)
 
-    for step in order:
-        wait_step((2,), step)
+    all_here(got_k.at[pl.ds(0, peers)], a_recv.at[2, 0])
     lax.fori_loop(1, gy + 1, spread_second, 0, unroll=8)
     strips_passed_on()
     lax.fori_loop(0, 2, lambda e, c: spread_second((gy + 1) * e, c), 0, unroll=2)
@@ -795,14 +786,12 @@
     coarse_sum3 = lax.fori_loop(0, tiles, third_coarse, zero, unroll=4)
 
     my_cols = pl.ds(pl.multiple_of(j * wide, LANES), wide)
-    finals = []
     for step in order:
         to = torus_add(j, step)
         copy = remote(
-            fin.at[to], coarse_out.at[:, :, my_cols], fin_send.at[step], fin_recv.at[step], i, to
+            fin.at[to], coarse_out.at[:, :, my_cols], fin_sem.at[0], fin_sem.at[1], i, to
         )
         copy.start()
-        finals.append(copy)
     for k in range(3):
         for t in range(halves):
             cols = pl.ds(pl.multiple_of(j * wide + LANES * t, LANES), LANES)
@@ -817,18 +806,16 @@
         line = jnp.sum(fine_part + coarse_part, axis=0, keepdims=True)
         mine = jnp.where(row_of == s, line, mine)
     part[0] = mine
-    norm_x = []
     for step in range(1, gx):
         copy = remote(
             part.at[0],
             part_gx.at[step],
-            norm_send.at[0, step],
-            norm_recv_x.at[step],
+            norm_sem.at[0],
+            norm_sem.at[1],
             lax.rem(i + step, gx),
             j,
         )
         copy.start()
-        norm_x.append(copy)
 
     def join_columns(k, carry):
         for b in range(sh.blocks):
@@ -843,25 +830,21 @@
 
     lax.fori_loop(0, 3, join_columns, 0)
 
-    for copy in norm_x:
-        copy.wait_recv()
+    all_here(part_gx.at[pl.ds(1, gx - 1)], norm_sem.at[1])
     for step in range(1, gx):
         mine = mine + part_gx[step]
     part[1] = mine
-    norm_y = []
     for step in order:
         copy = remote(
             part.at[1],
             part_gy.at[step],
-            norm_send.at[1, step],
-            norm_recv_y.at[step],
+            norm_sem.at[2],
+            norm_sem.at[3],
             i,
             torus_add(j, step),
         )
         copy.start()
-        norm_y.append(copy)
-    for copy in norm_y:
-        copy.wait_recv()
+    all_here(part_gy.at[pl.ds(1, peers)], norm_sem.at[3])
     for step in order:
         mine = mine + part_gy[step]
     total = jnp.sum(mine, axis=1, keepdims=True) * (1.0 / sh.cells)
@@ -887,19 +870,17 @@
             fwd_copies[kind][1].wait_send()
         strip_copies[1].wait_send()
 
-    for step in order:
-        for copy in sends[step]:
-            copy.wait_send()
+    for kind, ref in enumerate((got_c, got_p, got_k)):
+        all_sent(ref.at[pl.ds(0, peers)], a_send.at[kind])
 
     @pl.when((j == 0) | (j == gy - 1))
     def _():
-        for step in order:
-            strip_of(step, 0).wait_send()
-
-    for copy in finals:
-        copy.wait()
-    for copy in norm_y + norm_x:
-        copy.wait_send()
+        all_sent(strip_out.at[pl.ds(0, peers)], strip_send.at[0])
+
+    all_sent(fin.at[pl.ds(0, peers)], fin_sem.at[0])
+    all_here(fin.at[pl.ds(0, peers)], fin_sem.at[1])
+    all_sent(part_gx.at[pl.ds(1, gx - 1)], norm_sem.at[0])
+    all_sent(part_gy.at[pl.ds(1, peers)], norm_sem.at[2])
 
 
 def store_kernel(fine, coarse, norms, fine_out, coarse_out, norm_out, scalars, sem):
@@ -977,22 +958,19 @@
                 pltpu.VMEM((2, SUB, LANES), F32),
                 pltpu.VMEM((gy, SUB, LANES), F32),
                 pltpu.VMEM((gx, SUB, LANES), F32),
-                dma((3 + 3 * sh.slabs,)),
                 dma((2,)),
                 dma((2,)),
                 dma((2,)),
                 dma((2,)),
-                dma((3, gy)),
-                dma((3, gy)),
+                dma((2,)),
+                dma((3,)),
+                dma((3, 4)),
                 dma((2, 3)),
                 dma((2, 3)),
-                dma((gy,)),
+                dma((1,)),
                 dma((2,)),
-                dma((gy,)),
-                dma((gy,)),
-                dma((2, max(gx, gy))),
-                dma((gy,)),
-                dma((gx,)),
+                dma((2,)),
+                dma((4,)),
             ],
             compiler_params=pltpu.CompilerParams(
                 collective_id=0, has_side_effects=True, vmem_limit_bytes=64_500_000

time: 40.1 us -> 38.2 us (0.953)
  Pallas kernels: 39.4 us -> 37.5 us
    pallas_call x1, Pallas kernels: 38.1 us -> 36.2 us  [on_device(): pl.pallas_call(functools.partial(kernel, sh), out_shape=(pltpu.VMEM(fine_...]
where the time goes in v5:
time: 38.2 us; the launch traced here: 38.1 us
  Pallas kernels  37.5 us (98%)
  between operations  0.64 us (2%)
    pallas_call x1, Pallas kernels, on_device(): pl.pallas_call(functools.partial(kernel, sh), out_shape=(pltpu.VMEM(fine_...  36.2 us
    pallas_call x1, Pallas kernels, on_device(): pl.pallas_call(store_kernel, out_shape=(jax.ShapeDtypeStruct(fine_start.s...  1.3 us

profile of v5, /device:TPU:1, one launch (start us, length us, event | category | flops | bytes accessed | tf_op | source)
XLA Modules:
  0.0 38.1 jit_solution(15952847390808638225)
XLA Ops:
  0.6 36.2 %interface_sweeps.1 = (f32[3,256,512]{2,1,0:T(8,128)S(1)}, f32[3,8,4096]{2,1,0:T(8,128)S(1)}, f32[8,128]{1,0:T(8,128)S(1)}) custom-call(f32[3,256,512]{2,1,0:T(8,128)} %fine_start.1, f32[3,256,512]{2,1,0:T(8,128)} %fine_known.1, f32[256,512]{1,0:T(8,128)} %fine_mu.1, f32[3,8,4096]{2,1,0:T(8,128)} %coarse_start.1, f32[3,8,4096]{2,1,0:T(8,128)} %coarse_known.1, ...), custom_call_target="tpu_custom_call" | custom-call | tf_op jit(solution)/shard_map/interface_sweeps/pallas_call | solution.py:917
  36.8 1.3 %store_results.1 = (f32[3,256,512]{2,1,0:T(8,128)}, f32[3,8,4096]{2,1,0:T(8,128)}, f32[3]{0:T(128)}) custom-call(f32[3,256,512]{2,1,0:T(8,128)S(1)} %get-tuple-element.6.fine, f32[3,8,4096]{2,1,0:T(8,128)S(1)} %get-tuple-element.7.coarse, f32[8,128]{1,0:T(8,128)S(1)} %get-tuple-element.8.norms), custom_call_target="tpu_custom_call" | custom-call | tf_op jit(solution)/shard_map/store_results/pallas_call | solution.py:981

commit v6 on v5

--- a/solution.py
+++ b/solution.py
@@ -513,9 +513,10 @@
     lax.fori_loop(0, sh.fine_rows // (4 * SUB), diagonals, 0)
 
     for begin in range(0, gy, group):
-        if begin == gy // 2:
-            for step in order:
-                sends[step][2].start()
+        if begin in (0, gy // 2):
+            for step in order[::-1] if begin == 0 else order:
+                if (order.index(step) > 9) == (begin == 0):
+                    sends[step][2].start()
         steps = ([0] + order)[begin : begin + group]
         count = len(steps) - steps.count(0)
         all_here(got_c.at[pl.ds(0, count)], a_recv.at[0, begin // group])
@@ -884,18 +885,22 @@
 
 
 def store_kernel(fine, coarse, norms, fine_out, coarse_out, norm_out, scalars, sem):
+    half = fine.shape[1] // 2
+    for k in range(fine.shape[0]):
+        for part in range(2):
+            rows = pl.ds(half * part, half)
+            pltpu.make_async_copy(fine.at[k, rows], fine_out.at[k, rows], sem.at[0]).start()
     stores = [
-        pltpu.make_async_copy(fine, fine_out, sem.at[0]),
         pltpu.make_async_copy(coarse, coarse_out, sem.at[1]),
         pltpu.make_async_copy(scalars, norm_out, sem.at[2]),
     ]
     stores[0].start()
-    stores[1].start()
     for s in range(SWEEPS):
         scalars[s] = norms[s, 0]
-    stores[2].start()
+    stores[1].start()
     for copy in stores:
         copy.wait()
+    pltpu.make_async_copy(fine, fine_out, sem.at[0]).wait()
 
 
 def solution(mesh):
@@ -925,8 +930,8 @@
             out_specs=(on_chip, on_chip, on_chip),
             scratch_shapes=[
                 pltpu.VMEM((PLANES, sh.slabs, sh.fine_rows, LANES), F32),
-                pltpu.VMEM((PLANES, sh.blocks, sh.slabs * LANES, LANES), F32),
-                pltpu.VMEM((sh.blocks, sh.slabs * LANES, LANES), F32),
+                pltpu.VMEM((PLANES, sh.blocks, sh.slabs * LANES + SUB, LANES), F32),
+                pltpu.VMEM((sh.blocks, sh.slabs * LANES + SUB, LANES), F32),
                 fine(PLANES),
                 fine(3),
                 fine(),

time: 38.2 us -> 37.1 us (0.971)
  Pallas kernels: 37.5 us -> 36.3 us
    pallas_call x1, Pallas kernels: 36.2 us -> 35 us  [on_device(): pl.pallas_call(functools.partial(kernel, sh), out_shape=(pltpu.VMEM(fine_...]
where the time goes in v6:
time: 37.1 us; the launch traced here: 37 us
  Pallas kernels  36.3 us (98%)
  between operations  0.64 us (2%)
    pallas_call x1, Pallas kernels, on_device(): pl.pallas_call(functools.partial(kernel, sh), out_shape=(pltpu.VMEM(fine_...  35 us
    pallas_call x1, Pallas kernels, on_device(): pl.pallas_call(store_kernel, out_shape=(jax.ShapeDtypeStruct(fine_start.s...  1.3 us

profile of v6, /device:TPU:1, one launch (start us, length us, event | category | flops | bytes accessed | tf_op | source)
XLA Modules:
  0.0 37.0 jit_solution(15123269608204109075)
XLA Ops:
  0.6 35.0 %interface_sweeps.1 = (f32[3,256,512]{2,1,0:T(8,128)S(1)}, f32[3,8,4096]{2,1,0:T(8,128)S(1)}, f32[8,128]{1,0:T(8,128)S(1)}) custom-call(f32[3,256,512]{2,1,0:T(8,128)} %fine_start.1, f32[3,256,512]{2,1,0:T(8,128)} %fine_known.1, f32[256,512]{1,0:T(8,128)} %fine_mu.1, f32[3,8,4096]{2,1,0:T(8,128)} %coarse_start.1, f32[3,8,4096]{2,1,0:T(8,128)} %coarse_known.1, ...), custom_call_target="tpu_custom_call" | custom-call | tf_op jit(solution)/shard_map/interface_sweeps/pallas_call | solution.py:922
  35.7 1.3 %store_results.1 = (f32[3,256,512]{2,1,0:T(8,128)}, f32[3,8,4096]{2,1,0:T(8,128)}, f32[3]{0:T(128)}) custom-call(f32[3,256,512]{2,1,0:T(8,128)S(1)} %get-tuple-element.6.fine, f32[3,8,4096]{2,1,0:T(8,128)S(1)} %get-tuple-element.7.coarse, f32[8,128]{1,0:T(8,128)S(1)} %get-tuple-element.8.norms), custom_call_target="tpu_custom_call" | custom-call | tf_op jit(solution)/shard_map/store_results/pallas_call | solution.py:986

commit v7 on v6

--- a/solution.py
+++ b/solution.py
@@ -27,7 +27,7 @@
         self.tiles = self.coarse_rows // SUB
         self.halves = self.wide // LANES
         self.slabs = 2 * self.halves
-        self.fine_buf = fine_rows + 2 * FINE_OFF
+        self.fine_buf = fine_rows + 2 * FINE_OFF + SUB
         self.coarse_buf = self.coarse_rows + 2 * COARSE_OFF + SUB
         self.blocks = fine_rows // LANES
         self.cells = 3.0 * gx * gy * fine_rows * fine_cols * 1.25
@@ -784,7 +784,7 @@
     sums = lax.fori_loop(0, tiles, lead_and_follow, sums, unroll=4)
     sums = lax.fori_loop(tiles - 1, tiles + 1, follow, sums, unroll=2)
     coarse_sum1, fine_sum2, coarse_sum2 = sums
-    coarse_sum3 = lax.fori_loop(0, tiles, third_coarse, zero, unroll=4)
+    coarse_sum3 = lax.fori_loop(0, tiles, third_coarse, zero, unroll=8)
 
     my_cols = pl.ds(pl.multiple_of(j * wide, LANES), wide)
     for step in order:
@@ -798,7 +798,7 @@
             cols = pl.ds(pl.multiple_of(j * wide + LANES * t, LANES), LANES)
             coarse_out[k, :, cols] = fin[j, k, :, pl.ds(LANES * t, LANES)]
 
-    fine_sum3 = lax.fori_loop(0, tiles, fine_third, zero, unroll=8)
+    fine_sum3 = lax.fori_loop(0, tiles, fine_third, zero, unroll=16)
 
     row_of = lax.broadcasted_iota(jnp.int32, (SUB, LANES), 0)
     mine = zero

time: 37.1 us -> 36.8 us (level)
  no operation moved by 1% of the time
where the time goes in v7:
time: 36.8 us; the launch traced here: 36.7 us
  Pallas kernels  36 us (98%)
  between operations  0.64 us (2%)
    pallas_call x1, Pallas kernels, on_device(): pl.pallas_call(functools.partial(kernel, sh), out_shape=(pltpu.VMEM(fine_...  34.7 us
    pallas_call x1, Pallas kernels, on_device(): pl.pallas_call(store_kernel, out_shape=(jax.ShapeDtypeStruct(fine_start.s...  1.3 us

profile of v7, /device:TPU:1, one launch (start us, length us, event | category | flops | bytes accessed | tf_op | source)
XLA Modules:
  0.0 36.7 jit_solution(6285013551608347760)
XLA Ops:
  0.6 34.7 %interface_sweeps.1 = (f32[3,256,512]{2,1,0:T(8,128)S(1)}, f32[3,8,4096]{2,1,0:T(8,128)S(1)}, f32[8,128]{1,0:T(8,128)S(1)}) custom-call(f32[3,256,512]{2,1,0:T(8,128)} %fine_start.1, f32[3,256,512]{2,1,0:T(8,128)} %fine_known.1, f32[256,512]{1,0:T(8,128)} %fine_mu.1, f32[3,8,4096]{2,1,0:T(8,128)} %coarse_start.1, f32[3,8,4096]{2,1,0:T(8,128)} %coarse_known.1, ...), custom_call_target="tpu_custom_call" | custom-call | tf_op jit(solution)/shard_map/interface_sweeps/pallas_call | solution.py:922
  35.4 1.3 %store_results.1 = (f32[3,256,512]{2,1,0:T(8,128)}, f32[3,8,4096]{2,1,0:T(8,128)}, f32[3]{0:T(128)}) custom-call(f32[3,256,512]{2,1,0:T(8,128)S(1)} %get-tuple-element.6.fine, f32[3,8,4096]{2,1,0:T(8,128)S(1)} %get-tuple-element.7.coarse, f32[8,128]{1,0:T(8,128)S(1)} %get-tuple-element.8.norms), custom_call_target="tpu_custom_call" | custom-call | tf_op jit(solution)/shard_map/store_results/pallas_call | solution.py:986

commit v8 on v7

--- a/solution.py
+++ b/solution.py
@@ -716,7 +716,7 @@
         first_sum(m, 0)
         return fine_first(m, acc)
 
-    fine_sum1 = lax.fori_loop(1, tiles - 1, fine_first, zero, unroll=7)
+    fine_sum1 = lax.fori_loop(1, tiles - 1, fine_first, zero, unroll=14)
     lax.fori_loop(1, tiles - 1, first_sum, zero, unroll=7)
 
     @pl.when(has_up)
@@ -751,10 +751,10 @@
     fine_sum1 = lax.fori_loop(0, 2, outer_first, fine_sum1, unroll=2)
     every_tile(near_sum, zero)
 
+    strips_passed_on()
+    lax.fori_loop(0, 2, lambda e, c: spread_second((gy + 1) * e, c), 0, unroll=2)
     all_here(got_k.at[pl.ds(0, peers)], a_recv.at[2, 0])
     lax.fori_loop(1, gy + 1, spread_second, 0, unroll=8)
-    strips_passed_on()
-    lax.fori_loop(0, 2, lambda e, c: spread_second((gy + 1) * e, c), 0, unroll=2)
 
     @pl.when(has_down)
     def _():

time: 36.8 us -> 36.7 us (level)
  no operation moved by 1% of the time
where the time goes in v8:
time: 36.7 us; the launch traced here: 36.6 us
  Pallas kernels  35.9 us (98%)
  between operations  0.64 us (2%)
    pallas_call x1, Pallas kernels, on_device(): pl.pallas_call(functools.partial(kernel, sh), out_shape=(pltpu.VMEM(fine_...  34.6 us
    pallas_call x1, Pallas kernels, on_device(): pl.pallas_call(store_kernel, out_shape=(jax.ShapeDtypeStruct(fine_start.s...  1.3 us

profile of v8, /device:TPU:1, one launch (start us, length us, event | category | flops | bytes accessed | tf_op | source)
XLA Modules:
  0.0 36.6 jit_solution(4612561649867985996)
XLA Ops:
  0.6 34.6 %interface_sweeps.1 = (f32[3,256,512]{2,1,0:T(8,128)S(1)}, f32[3,8,4096]{2,1,0:T(8,128)S(1)}, f32[8,128]{1,0:T(8,128)S(1)}) custom-call(f32[3,256,512]{2,1,0:T(8,128)} %fine_start.1, f32[3,256,512]{2,1,0:T(8,128)} %fine_known.1, f32[256,512]{1,0:T(8,128)} %fine_mu.1, f32[3,8,4096]{2,1,0:T(8,128)} %coarse_start.1, f32[3,8,4096]{2,1,0:T(8,128)} %coarse_known.1, ...), custom_call_target="tpu_custom_call" | custom-call | tf_op jit(solution)/shard_map/interface_sweeps/pallas_call | solution.py:922
  35.3 1.3 %store_results.1 = (f32[3,256,512]{2,1,0:T(8,128)}, f32[3,8,4096]{2,1,0:T(8,128)}, f32[3]{0:T(128)}) custom-call(f32[3,256,512]{2,1,0:T(8,128)S(1)} %get-tuple-element.6.fine, f32[3,8,4096]{2,1,0:T(8,128)S(1)} %get-tuple-element.7.coarse, f32[8,128]{1,0:T(8,128)S(1)} %get-tuple-element.8.norms), custom_call_target="tpu_custom_call" | custom-call | tf_op jit(solution)/shard_map/store_results/pallas_call | solution.py:986
